TPU v7x, 32 devices: a whole 2x2x4 slice. The times are simulated.
32 devices in a mesh: parts: 2 (over y), row: 4 (over z), col: 4 (over x, core).
Axes of the slice: x: 2, y: 2, z: 4, core: 2. Of those that a mesh axis runs over, the one named last changes fastest.
Arguments:
- state: float32 [10, 128, 512], P(None, ('parts', 'row'), 'col'), parts along dimension 1, may hold values from -5 to 5
- history: float32 [10, 128, 512], P(None, ('parts', 'row'), 'col'), parts along dimension 1, may hold values from -5 to 5
- rates: float32 [10, 10, 128, 512], P(None, None, ('parts', 'row'), 'col'), parts along dimension 2, may hold values from -2 to 2
- quadratic: float32 [10, 128, 512], P(None, ('parts', 'row'), 'col'), parts along dimension 1, may hold values from 0.1 to 1
- velocity: float32 [10, 2], replicated, may hold values from -1.5 to 1.5
- precond: float32 [10, 10, 128, 512], P(None, None, ('parts', 'row'), 'col'), parts along dimension 2, may hold values from -1 to 2, as said below
Outputs:
- updated: float32 [10, 128, 512], P(None, ('parts', 'row'), 'col'), parts along dimension 1
- lin_residual: float32 [2], P('parts'), parts along dimension 0
There are 2 independent parts, one for each index of `parts`. A program takes and returns all parts, laid end to end along the dimension named above; an argument that names none is the same for every part. Nothing has to cross between parts.
Inputs may be any that keep to these rules, and one draw needn't show every extreme that they name: `precond`: each cell's block has diagonal entries 1 plus a spread term and independent off-diagonal entries.
All inputs are finite; a program needn't handle non-finite values.
Results may differ from a plain program's by a relative error of at most 0.00011.
Values sent between devices are 32-bit elements; how exact they have to be, the bound alone decides.
No kernel may reach another device: no remote copies, remote signals or barrier semaphores. Data moves between devices by JAX's collectives and lax.ppermute only.
A program may use at most 64 MiB of HBM per device.

v0:
```python
import jax
import jax.numpy as jnp
from jax import lax
from jax.sharding import PartitionSpec as P

KRYLOV = 4


step_gamma = 0.4
tiny_eps = 1e-12


def extended(block, sides, width):
    for axis, dim in sides:
        count = lax.axis_size(axis)
        forward = [(i, i + 1) for i in range(count - 1)]
        backward = [(target, source) for source, target in forward]
        low = lax.ppermute(
            lax.slice_in_dim(block, block.shape[dim] - width, None, axis=dim), axis, forward
        )
        high = lax.ppermute(lax.slice_in_dim(block, 0, width, axis=dim), axis, backward)
        block = jnp.concatenate([low, block, high], axis=dim)
    return block


def advect(field, velocity):
    padded = extended(field, (("row", 1), ("col", 2)), 1)
    along_x = padded[:, 2:, 1:-1] - padded[:, :-2, 1:-1]
    along_y = padded[:, 1:-1, 2:] - padded[:, 1:-1, :-2]
    return -0.5 * (
        velocity[:, 0][:, None, None] * along_x + velocity[:, 1][:, None, None] * along_y
    )


def blockmul(matrix, field):
    return jnp.sum(matrix * field[None], axis=1)


def least_squares(hessen, beta):
    width = hessen.shape[1]
    rotated = jnp.zeros((width + 1,), jnp.float32).at[0].set(beta)
    upper = hessen
    for index in range(width):
        first = upper[index, index]
        second = upper[index + 1, index]
        radius = jnp.sqrt(first * first + second * second)
        cosine = first / radius
        sine = second / radius
        row_top = cosine * upper[index] + sine * upper[index + 1]
        row_low = -sine * upper[index] + cosine * upper[index + 1]
        upper = upper.at[index].set(row_top).at[index + 1].set(row_low)
        g_top = cosine * rotated[index] + sine * rotated[index + 1]
        g_low = -sine * rotated[index] + cosine * rotated[index + 1]
        rotated = rotated.at[index].set(g_top).at[index + 1].set(g_low)
    coef = jnp.zeros((width,), jnp.float32)
    for index in reversed(range(width)):
        partial_sum = jnp.sum(upper[index, index + 1 : width] * coef[index + 1 : width])
        coef = coef.at[index].set((rotated[index] - partial_sum) / upper[index, index])
    return (coef, jnp.abs(rotated[width]))


def body(state, history, rates, quadratic, velocity, precond):
    forcing = advect(state, velocity) + blockmul(rates, state) - quadratic * state * state
    rhs = -(state - history - step_gamma * forcing)
    beta = jnp.sqrt(lax.psum(jnp.sum(rhs * rhs), ("row", "col")) + tiny_eps)
    basis = [rhs / beta]
    kept = []
    hessen = jnp.zeros((KRYLOV + 1, KRYLOV), jnp.float32)
    for index in range(KRYLOV):
        direct = blockmul(precond, basis[index])
        kept.append(direct)
        jac = advect(direct, velocity) + blockmul(rates, direct) - 2.0 * quadratic * state * direct
        vector = direct - step_gamma * jac
        stacked = jnp.stack(basis)
        local_dots = jnp.sum(stacked * vector[None], axis=(1, 2, 3))
        dots, before = lax.psum((local_dots, jnp.sum(vector * vector)), ("row", "col"))
        vector = vector - jnp.sum(dots[:, None, None, None] * stacked, axis=0)
        squared = before - jnp.sum(dots * dots)
        size_new = jnp.sqrt(squared + tiny_eps)
        hessen = hessen.at[: index + 1, index].set(dots).at[index + 1, index].set(size_new)
        basis.append(vector / size_new)
    coef, lin_norm = least_squares(hessen, beta)
    combined = jnp.sum(coef[:, None, None, None] * jnp.stack(basis[:KRYLOV]), axis=0)
    correction = blockmul(precond, combined)
    return (state + correction, jnp.reshape(lin_norm, (1,)))


def solution(mesh):
    placed = (
        P(None, ("parts", "row"), "col"),
        P(None, ("parts", "row"), "col"),
        P(None, None, ("parts", "row"), "col"),
        P(None, ("parts", "row"), "col"),
        P(),
        P(None, None, ("parts", "row"), "col"),
    )
    return jax.shard_map(
        body,
        mesh=mesh,
        in_specs=placed,
        out_specs=(P(None, ("parts", "row"), "col"), P("parts")),
        check_vma=False,
    )
```

profile of v0, /device:TPU:0, one launch (start us, length us, event | category | flops | bytes accessed | tf_op | source)
XLA Modules:
  0.0 279.6 jit_solution(16215169505555502827)
XLA Ops:
  0.6 0.8 fusion.64
  1.4 1.3 collective-permute-start
  2.7 5.6 %collective-permute-start.1 = (f32[10,1,128]{2,1,0:T(1,128)S(1)}, f32[10,1,128]{2,1,0:T(1,128)S(1)}, u32[]{:S(2)}, u32[]{:S(2)}) collective-permute-start(f32[10,1,128]{2,1,0:T(1,128)S(1)} %get-tuple-element.388), channel_id=1, source_target_pairs={{0,4},{4,8},{8,12},{1,5},{5,9},{9,13},{2,6},{6,10},{10,14},{3,7},{... | collective-permute-start | bytes 15368 | tf_op jit(solution)/shard_map/ppermute | solution.py:18
  8.4 1.3 multiply_reduce_fusion.9
  9.7 0.6 fusion.71
  10.3 0.7 and_reduce_fusion.1
  11.0 0.7 and_reduce_fusion
  11.8 0.6 fusion.70
  12.5 1.3 collective-permute-start.2
  13.8 3.0 %collective-permute-start.3 = (f32[10,18,1]{2,1,0:T(8,128)S(1)}, f32[10,18,1]{2,1,0:T(8,128)S(1)}, u32[]{:S(2)}, u32[]{:S(2)}) collective-permute-start(f32[10,18,1]{2,1,0:T(8,128)S(1)} %get-tuple-element.379), channel_id=1, source_target_pairs={{0,1},{1,2},{2,3},{4,5},{5,6},{6,7},{8,9},{9,10},{10,11},{12,13},{... | collective-permute-start | bytes 2168 | tf_op jit(solution)/shard_map/ppermute | solution.py:18
  16.9 0.9 collective-permute-done.3
  17.8 0.8 multiply_reduce_fusion.21
  18.6 33.0 %psum.63 = f32[]{:T(128)} all-reduce(f32[]{:T(128)} %get-tuple-element.368), channel_id=1, replica_groups=mesh['parts'=2,'row'=4,'col'=4] {'row','col'}, use_global_device_ids=true, to_apply=%region_2.0 | all-reduce | flops 1 | bytes 8 | tf_op jit(solution)/shard_map/psum | solution.py:65
  52.4 1.4 collective-permute-start.4
  53.9 4.5 %collective-permute-start.5 = (f32[10,1,128]{2,1,0:T(1,128)S(1)}, f32[10,1,128]{2,1,0:T(1,128)S(1)}, u32[]{:S(2)}, u32[]{:S(2)}) collective-permute-start(f32[10,1,128]{2,1,0:T(1,128)S(1)} %get-tuple-element.386), channel_id=1, source_target_pairs={{0,4},{4,8},{8,12},{1,5},{5,9},{9,13},{2,6},{6,10},{10,14},{3,7},{... | collective-permute-start | bytes 15368 | tf_op jit(solution)/shard_map/ppermute | solution.py:18
  58.4 0.6 fusion.69
  59.0 0.6 compare_reduce_fusion
  59.9 1.3 collective-permute-start.6
  61.2 3.0 %collective-permute-start.7 = (f32[10,18,1]{2,1,0:T(8,128)S(1)}, f32[10,18,1]{2,1,0:T(8,128)S(1)}, u32[]{:S(2)}, u32[]{:S(2)}) collective-permute-start(f32[10,18,1]{2,1,0:T(8,128)S(1)} %get-tuple-element.377), channel_id=1, source_target_pairs={{0,1},{1,2},{2,3},{4,5},{5,6},{6,7},{8,9},{9,10},{10,11},{12,13},{... | collective-permute-start | bytes 2168 | tf_op jit(solution)/shard_map/ppermute | solution.py:18
  64.3 0.9 collective-permute-done.7
  65.2 0.8 multiply_reduce_fusion.20
  66.0 31.1 %all-reduce.6 = (f32[]{:T(128)}, f32[1]{0:T(128)}) all-reduce(f32[]{:T(128)} %get-tuple-element.351, f32[1]{0:T(128)} %bitcast.2), channel_id=1, replica_groups=mesh['parts'=2,'row'=4,'col'=4] {'row','col'}, use_global_device_ids=true, to_apply=%region_8.0 | all-reduce | flops 2 | bytes 16 | tf_op jit(solution)/shard_map/psum | solution.py:76
  99.1 0.7 subtract_divide_fusion.2
  99.8 1.3 collective-permute-start.8
  101.1 4.5 %collective-permute-start.9 = (f32[10,1,128]{2,1,0:T(1,128)S(1)}, f32[10,1,128]{2,1,0:T(1,128)S(1)}, u32[]{:S(2)}, u32[]{:S(2)}) collective-permute-start(f32[10,1,128]{2,1,0:T(1,128)S(1)} %get-tuple-element.384), channel_id=1, source_target_pairs={{0,4},{4,8},{8,12},{1,5},{5,9},{9,13},{2,6},{6,10},{10,14},{3,7},{... | collective-permute-start | bytes 15368 | tf_op jit(solution)/shard_map/ppermute | solution.py:18
  105.7 1.3 collective-permute-done.9
  107.1 1.3 collective-permute-start.10
  108.4 3.0 %collective-permute-start.11 = (f32[10,18,1]{2,1,0:T(8,128)S(1)}, f32[10,18,1]{2,1,0:T(8,128)S(1)}, u32[]{:S(2)}, u32[]{:S(2)}) collective-permute-start(f32[10,18,1]{2,1,0:T(8,128)S(1)} %get-tuple-element.375), channel_id=1, source_target_pairs={{0,1},{1,2},{2,3},{4,5},{5,6},{6,7},{8,9},{9,10},{10,11},{12,13},{... | collective-permute-start | bytes 2168 | tf_op jit(solution)/shard_map/ppermute | solution.py:18
  111.6 0.7 scatter.56
  112.4 0.8 multiply_reduce_fusion.18
  113.3 31.0 %all-reduce.5 = (f32[2]{0:T(128)S(1)}, f32[]{:T(128)}) all-reduce(f32[2]{0:T(128)S(1)} %multiply_reduce_fusion.15, f32[]{:T(128)} %get-tuple-element.364), channel_id=1, replica_groups=mesh['parts'=2,'row'=4,'col'=4] {'row','col'}, use_global_device_ids=true, to_apply=%region_13.0 | all-reduce | flops 3 | bytes 24 | tf_op jit(solution)/shard_map/psum | solution.py:76
  144.4 0.7 multiply_reduce_fusion.26
  146.6 1.3 collective-permute-start.12
  147.9 4.5 %collective-permute-start.13 = (f32[10,1,128]{2,1,0:T(1,128)S(1)}, f32[10,1,128]{2,1,0:T(1,128)S(1)}, u32[]{:S(2)}, u32[]{:S(2)}) collective-permute-start(f32[10,1,128]{2,1,0:T(1,128)S(1)} %get-tuple-element.382), channel_id=1, source_target_pairs={{0,4},{4,8},{8,12},{1,5},{5,9},{9,13},{2,6},{6,10},{10,14},{3,7},{... | collective-permute-start | bytes 15368 | tf_op jit(solution)/shard_map/ppermute | solution.py:18
  152.4 1.9 broadcast_select_fusion.2
  154.4 1.3 collective-permute-start.14
  155.8 3.0 %collective-permute-start.15 = (f32[10,18,1]{2,1,0:T(8,128)S(1)}, f32[10,18,1]{2,1,0:T(8,128)S(1)}, u32[]{:S(2)}, u32[]{:S(2)}) collective-permute-start(f32[10,18,1]{2,1,0:T(8,128)S(1)} %get-tuple-element.373), channel_id=1, source_target_pairs={{0,1},{1,2},{2,3},{4,5},{5,6},{6,7},{8,9},{9,10},{10,11},{12,13},{... | collective-permute-start | bytes 2168 | tf_op jit(solution)/shard_map/ppermute | solution.py:18
  158.9 1.4 scatter.60
  160.4 0.8 multiply_reduce_fusion.17
  161.3 30.3 %all-reduce.4 = (f32[3]{0:T(128)S(1)}, f32[]{:T(128)}) all-reduce(f32[3]{0:T(128)S(1)} %multiply_reduce_fusion.13, f32[]{:T(128)} %get-tuple-element.362), channel_id=1, replica_groups=mesh['parts'=2,'row'=4,'col'=4] {'row','col'}, use_global_device_ids=true, to_apply=%region_22.0 | all-reduce | flops 4 | bytes 32 | tf_op jit(solution)/shard_map/psum | solution.py:76
  191.7 0.6 multiply_reduce_fusion.25
  193.7 1.3 collective-permute-start.16
  195.0 4.5 %collective-permute-start.17 = (f32[10,1,128]{2,1,0:T(1,128)S(1)}, f32[10,1,128]{2,1,0:T(1,128)S(1)}, u32[]{:S(2)}, u32[]{:S(2)}) collective-permute-start(f32[10,1,128]{2,1,0:T(1,128)S(1)} %get-tuple-element.380), channel_id=1, source_target_pairs={{0,4},{4,8},{8,12},{1,5},{5,9},{9,13},{2,6},{6,10},{10,14},{3,7},{... | collective-permute-start | bytes 15368 | tf_op jit(solution)/shard_map/ppermute | solution.py:18
  199.6 1.9 broadcast_select_fusion.1
  201.6 1.3 collective-permute-start.18
  202.9 3.0 %collective-permute-start.19 = (f32[10,18,1]{2,1,0:T(8,128)S(1)}, f32[10,18,1]{2,1,0:T(8,128)S(1)}, u32[]{:S(2)}, u32[]{:S(2)}) collective-permute-start(f32[10,18,1]{2,1,0:T(8,128)S(1)} %get-tuple-element.371), channel_id=1, source_target_pairs={{0,1},{1,2},{2,3},{4,5},{5,6},{6,7},{8,9},{9,10},{10,11},{12,13},{... | collective-permute-start | bytes 2168 | tf_op jit(solution)/shard_map/ppermute | solution.py:18
  206.0 1.4 scatter.64
  207.6 0.8 multiply_reduce_fusion.16
  208.5 30.7 %all-reduce.3 = (f32[4]{0:T(128)S(1)}, f32[]{:T(128)}) all-reduce(f32[4]{0:T(128)S(1)} %multiply_reduce_fusion.11, f32[]{:T(128)} %get-tuple-element.360), channel_id=1, replica_groups=mesh['parts'=2,'row'=4,'col'=4] {'row','col'}, use_global_device_ids=true, to_apply=%region_31.0 | all-reduce | flops 5 | bytes 40 | tf_op jit(solution)/shard_map/psum | solution.py:76
  239.2 0.7 multiply_reduce_fusion.24
  241.1 2.0 broadcast_select_fusion
  243.1 1.3 scatter.66
  244.6 0.7 fusion.67
  249.4 0.7 fusion.66
  254.4 0.5 slice.739
  259.0 0.5 slice.741
  263.5 0.6 slice.745
  265.4 0.6 fusion.68
  268.6 0.5 slice.756
  269.8 0.5 slice.750
  270.3 0.6 fusion.65
  272.9 0.7 multiply_reduce_fusion.23
  275.0 0.7 multiply_reduce_fusion.22
  277.8 0.6 add.240
  (91 shorter events, 4.4 us)
Async XLA Ops:
  1.4 10.9 %collective-permute-start = (f32[10,1,128]{2,1,0:T(1,128)S(1)}, f32[10,1,128]{2,1,0:T(1,128)S(1)}, u32[]{:S(2)}, u32[]{:S(2)}) collective-permute-start(f32[10,1,128]{2,1,0:T(1,128)S(1)} %get-tuple-element.389), channel_id=1, source_target_pairs={{4,0},{8,4},{12,8},{5,1},{9,5},{13,9},{6,2},{10,6},{14,10},{7,3},{... | collective-permute-start | bytes 15368 | tf_op jit(solution)/shard_map/ppermute | solution.py:21
  2.7 5.6 %copy-start.5 = (f32[10,2]{0,1:T(2,128)S(1)}, f32[10,2]{0,1:T(2,128)}, u32[]{:S(2)}) copy-start(f32[10,2]{0,1:T(2,128)} %param.68) | copy-start | bytes 244
  2.7 9.6 %collective-permute-start.1 = (f32[10,1,128]{2,1,0:T(1,128)S(1)}, f32[10,1,128]{2,1,0:T(1,128)S(1)}, u32[]{:S(2)}, u32[]{:S(2)}) collective-permute-start(f32[10,1,128]{2,1,0:T(1,128)S(1)} %get-tuple-element.388), channel_id=1, source_target_pairs={{0,4},{4,8},{8,12},{1,5},{5,9},{9,13},{2,6},{6,10},{10,14},{3,7},{... | collective-permute-start | bytes 15368 | tf_op jit(solution)/shard_map/ppermute | solution.py:18
  8.4 2.0 copy-start.6
  8.4 2.7 copy-start.7
  8.4 4.0 %copy-start.2 = (f32[10,16,128]{2,1,0:T(8,128)S(1)}, f32[10,16,128]{2,1,0:T(8,128)}, u32[]{:S(2)}) copy-start(f32[10,16,128]{2,1,0:T(8,128)} %param.64) | copy-start | bytes 245764
  8.4 9.4 %copy-start.3 = (f32[10,16,128]{2,1,0:T(8,128)S(1)}, f32[10,16,128]{2,1,0:T(8,128)}, u32[]{:S(2)}) copy-start(f32[10,16,128]{2,1,0:T(8,128)} %param.67) | copy-start | bytes 245764
  8.4 9.4 %copy-start.4 = (f32[10,16,128]{2,1,0:T(8,128)S(1)}, f32[10,16,128]{2,1,0:T(8,128)}, u32[]{:S(2)}) copy-start(f32[10,16,128]{2,1,0:T(8,128)} %param.65) | copy-start | bytes 245764
  9.7 42.6 %copy-start.1 = (f32[10,10,16,128]{3,2,1,0:T(8,128)S(1)}, f32[10,10,16,128]{3,2,1,0:T(8,128)}, u32[]{:S(2)}) copy-start(f32[10,10,16,128]{3,2,1,0:T(8,128)} %param.69) | copy-start | bytes 2457604
  12.5 4.4 %collective-permute-start.2 = (f32[10,18,1]{2,1,0:T(8,128)S(1)}, f32[10,18,1]{2,1,0:T(8,128)S(1)}, u32[]{:S(2)}, u32[]{:S(2)}) collective-permute-start(f32[10,18,1]{2,1,0:T(8,128)S(1)} %get-tuple-element.378), channel_id=1, source_target_pairs={{1,0},{2,1},{3,2},{5,4},{6,5},{7,6},{9,8},{10,9},{11,10},{13,12},{... | collective-permute-start | bytes 2168 | tf_op jit(solution)/shard_map/ppermute | solution.py:21
  13.8 4.0 %collective-permute-start.3 = (f32[10,18,1]{2,1,0:T(8,128)S(1)}, f32[10,18,1]{2,1,0:T(8,128)S(1)}, u32[]{:S(2)}, u32[]{:S(2)}) collective-permute-start(f32[10,18,1]{2,1,0:T(8,128)S(1)} %get-tuple-element.379), channel_id=1, source_target_pairs={{0,1},{1,2},{2,3},{4,5},{5,6},{6,7},{8,9},{9,10},{10,11},{12,13},{... | collective-permute-start | bytes 2168 | tf_op jit(solution)/shard_map/ppermute | solution.py:18
  52.3 11.9 %copy-start = (f32[10,10,16,128]{3,2,1,0:T(8,128)S(1)}, f32[10,10,16,128]{3,2,1,0:T(8,128)}, u32[]{:S(2)}) copy-start(f32[10,10,16,128]{3,2,1,0:T(8,128)} %param.66) | copy-start | bytes 2457604
  52.4 7.2 %collective-permute-start.4 = (f32[10,1,128]{2,1,0:T(1,128)S(1)}, f32[10,1,128]{2,1,0:T(1,128)S(1)}, u32[]{:S(2)}, u32[]{:S(2)}) collective-permute-start(f32[10,1,128]{2,1,0:T(1,128)S(1)} %get-tuple-element.387), channel_id=1, source_target_pairs={{4,0},{8,4},{12,8},{5,1},{9,5},{13,9},{6,2},{10,6},{14,10},{7,3},{... | collective-permute-start | bytes 15368 | tf_op jit(solution)/shard_map/ppermute | solution.py:21
  53.9 5.9 %collective-permute-start.5 = (f32[10,1,128]{2,1,0:T(1,128)S(1)}, f32[10,1,128]{2,1,0:T(1,128)S(1)}, u32[]{:S(2)}, u32[]{:S(2)}) collective-permute-start(f32[10,1,128]{2,1,0:T(1,128)S(1)} %get-tuple-element.386), channel_id=1, source_target_pairs={{0,4},{4,8},{8,12},{1,5},{5,9},{9,13},{2,6},{6,10},{10,14},{3,7},{... | collective-permute-start | bytes 15368 | tf_op jit(solution)/shard_map/ppermute | solution.py:18
  59.9 4.4 %collective-permute-start.6 = (f32[10,18,1]{2,1,0:T(8,128)S(1)}, f32[10,18,1]{2,1,0:T(8,128)S(1)}, u32[]{:S(2)}, u32[]{:S(2)}) collective-permute-start(f32[10,18,1]{2,1,0:T(8,128)S(1)} %get-tuple-element.376), channel_id=1, source_target_pairs={{1,0},{2,1},{3,2},{5,4},{6,5},{7,6},{9,8},{10,9},{11,10},{13,12},{... | collective-permute-start | bytes 2168 | tf_op jit(solution)/shard_map/ppermute | solution.py:21
  61.2 4.0 %collective-permute-start.7 = (f32[10,18,1]{2,1,0:T(8,128)S(1)}, f32[10,18,1]{2,1,0:T(8,128)S(1)}, u32[]{:S(2)}, u32[]{:S(2)}) collective-permute-start(f32[10,18,1]{2,1,0:T(8,128)S(1)} %get-tuple-element.377), channel_id=1, source_target_pairs={{0,1},{1,2},{2,3},{4,5},{5,6},{6,7},{8,9},{9,10},{10,11},{12,13},{... | collective-permute-start | bytes 2168 | tf_op jit(solution)/shard_map/ppermute | solution.py:18
  99.8 5.9 %collective-permute-start.8 = (f32[10,1,128]{2,1,0:T(1,128)S(1)}, f32[10,1,128]{2,1,0:T(1,128)S(1)}, u32[]{:S(2)}, u32[]{:S(2)}) collective-permute-start(f32[10,1,128]{2,1,0:T(1,128)S(1)} %get-tuple-element.385), channel_id=1, source_target_pairs={{4,0},{8,4},{12,8},{5,1},{9,5},{13,9},{6,2},{10,6},{14,10},{7,3},{... | collective-permute-start | bytes 15368 | tf_op jit(solution)/shard_map/ppermute | solution.py:21
  101.1 5.9 %collective-permute-start.9 = (f32[10,1,128]{2,1,0:T(1,128)S(1)}, f32[10,1,128]{2,1,0:T(1,128)S(1)}, u32[]{:S(2)}, u32[]{:S(2)}) collective-permute-start(f32[10,1,128]{2,1,0:T(1,128)S(1)} %get-tuple-element.384), channel_id=1, source_target_pairs={{0,4},{4,8},{8,12},{1,5},{5,9},{9,13},{2,6},{6,10},{10,14},{3,7},{... | collective-permute-start | bytes 15368 | tf_op jit(solution)/shard_map/ppermute | solution.py:18
  107.1 5.2 %collective-permute-start.10 = (f32[10,18,1]{2,1,0:T(8,128)S(1)}, f32[10,18,1]{2,1,0:T(8,128)S(1)}, u32[]{:S(2)}, u32[]{:S(2)}) collective-permute-start(f32[10,18,1]{2,1,0:T(8,128)S(1)} %get-tuple-element.374), channel_id=1, source_target_pairs={{1,0},{2,1},{3,2},{5,4},{6,5},{7,6},{9,8},{10,9},{11,10},{13,12},{... | collective-permute-start | bytes 2168 | tf_op jit(solution)/shard_map/ppermute | solution.py:21
  108.4 4.0 %collective-permute-start.11 = (f32[10,18,1]{2,1,0:T(8,128)S(1)}, f32[10,18,1]{2,1,0:T(8,128)S(1)}, u32[]{:S(2)}, u32[]{:S(2)}) collective-permute-start(f32[10,18,1]{2,1,0:T(8,128)S(1)} %get-tuple-element.375), channel_id=1, source_target_pairs={{0,1},{1,2},{2,3},{4,5},{5,6},{6,7},{8,9},{9,10},{10,11},{12,13},{... | collective-permute-start | bytes 2168 | tf_op jit(solution)/shard_map/ppermute | solution.py:18
  146.6 7.7 %collective-permute-start.12 = (f32[10,1,128]{2,1,0:T(1,128)S(1)}, f32[10,1,128]{2,1,0:T(1,128)S(1)}, u32[]{:S(2)}, u32[]{:S(2)}) collective-permute-start(f32[10,1,128]{2,1,0:T(1,128)S(1)} %get-tuple-element.383), channel_id=1, source_target_pairs={{4,0},{8,4},{12,8},{5,1},{9,5},{13,9},{6,2},{10,6},{14,10},{7,3},{... | collective-permute-start | bytes 15368 | tf_op jit(solution)/shard_map/ppermute | solution.py:21
  147.9 6.4 %collective-permute-start.13 = (f32[10,1,128]{2,1,0:T(1,128)S(1)}, f32[10,1,128]{2,1,0:T(1,128)S(1)}, u32[]{:S(2)}, u32[]{:S(2)}) collective-permute-start(f32[10,1,128]{2,1,0:T(1,128)S(1)} %get-tuple-element.382), channel_id=1, source_target_pairs={{0,4},{4,8},{8,12},{1,5},{5,9},{9,13},{2,6},{6,10},{10,14},{3,7},{... | collective-permute-start | bytes 15368 | tf_op jit(solution)/shard_map/ppermute | solution.py:18
  154.4 6.0 %collective-permute-start.14 = (f32[10,18,1]{2,1,0:T(8,128)S(1)}, f32[10,18,1]{2,1,0:T(8,128)S(1)}, u32[]{:S(2)}, u32[]{:S(2)}) collective-permute-start(f32[10,18,1]{2,1,0:T(8,128)S(1)} %get-tuple-element.372), channel_id=1, source_target_pairs={{1,0},{2,1},{3,2},{5,4},{6,5},{7,6},{9,8},{10,9},{11,10},{13,12},{... | collective-permute-start | bytes 2168 | tf_op jit(solution)/shard_map/ppermute | solution.py:21
  155.8 4.7 %collective-permute-start.15 = (f32[10,18,1]{2,1,0:T(8,128)S(1)}, f32[10,18,1]{2,1,0:T(8,128)S(1)}, u32[]{:S(2)}, u32[]{:S(2)}) collective-permute-start(f32[10,18,1]{2,1,0:T(8,128)S(1)} %get-tuple-element.373), channel_id=1, source_target_pairs={{0,1},{1,2},{2,3},{4,5},{5,6},{6,7},{8,9},{9,10},{10,11},{12,13},{... | collective-permute-start | bytes 2168 | tf_op jit(solution)/shard_map/ppermute | solution.py:18
  193.7 7.8 %collective-permute-start.16 = (f32[10,1,128]{2,1,0:T(1,128)S(1)}, f32[10,1,128]{2,1,0:T(1,128)S(1)}, u32[]{:S(2)}, u32[]{:S(2)}) collective-permute-start(f32[10,1,128]{2,1,0:T(1,128)S(1)} %get-tuple-element.381), channel_id=1, source_target_pairs={{4,0},{8,4},{12,8},{5,1},{9,5},{13,9},{6,2},{10,6},{14,10},{7,3},{... | collective-permute-start | bytes 15368 | tf_op jit(solution)/shard_map/ppermute | solution.py:21
  195.0 6.5 %collective-permute-start.17 = (f32[10,1,128]{2,1,0:T(1,128)S(1)}, f32[10,1,128]{2,1,0:T(1,128)S(1)}, u32[]{:S(2)}, u32[]{:S(2)}) collective-permute-start(f32[10,1,128]{2,1,0:T(1,128)S(1)} %get-tuple-element.380), channel_id=1, source_target_pairs={{0,4},{4,8},{8,12},{1,5},{5,9},{9,13},{2,6},{6,10},{10,14},{3,7},{... | collective-permute-start | bytes 15368 | tf_op jit(solution)/shard_map/ppermute | solution.py:18
  201.6 5.9 %collective-permute-start.18 = (f32[10,18,1]{2,1,0:T(8,128)S(1)}, f32[10,18,1]{2,1,0:T(8,128)S(1)}, u32[]{:S(2)}, u32[]{:S(2)}) collective-permute-start(f32[10,18,1]{2,1,0:T(8,128)S(1)} %get-tuple-element.370), channel_id=1, source_target_pairs={{1,0},{2,1},{3,2},{5,4},{6,5},{7,6},{9,8},{10,9},{11,10},{13,12},{... | collective-permute-start | bytes 2168 | tf_op jit(solution)/shard_map/ppermute | solution.py:21
  202.9 4.6 %collective-permute-start.19 = (f32[10,18,1]{2,1,0:T(8,128)S(1)}, f32[10,18,1]{2,1,0:T(8,128)S(1)}, u32[]{:S(2)}, u32[]{:S(2)}) collective-permute-start(f32[10,18,1]{2,1,0:T(8,128)S(1)} %get-tuple-element.371), channel_id=1, source_target_pairs={{0,1},{1,2},{2,3},{4,5},{5,6},{6,7},{8,9},{9,10},{10,11},{12,13},{... | collective-permute-start | bytes 2168 | tf_op jit(solution)/shard_map/ppermute | solution.py:18
where the time goes:
time: 281 us; the launch traced here: 280 us
  blocking collectives  156 us (56%)
  starting transfers between devices  52 us (19%)
  between operations  33.8 us (12%)
  other arithmetic  19.4 us (7%)
  local copies, waits for them, and re-layouts  15 us (5%)
  waiting for transfers between devices  3.3 us (1%)
    psum x4, blocking collectives, body(): lax.psum((local_dots, jnp.sum(vector * vector)), ('row', 'col'))  123 us
    ppermute x10, starting transfers between devices, extended(): lax.ppermute(lax.slice_in_dim(block, block.shape[dim] - width, None, axis...  39 us
    psum x1, blocking collectives, body(): beta = jnp.sqrt(lax.psum(jnp.sum(rhs * rhs), ('row', 'col')) + tiny_eps)  33 us
    ppermute x10, starting transfers between devices, extended(): lax.ppermute(lax.slice_in_dim(block, 0, width, axis=dim), axis, backward)  13 us
    another operation x8, other arithmetic  7.82 us
  transfers between devices with their start and end apart: 20, of which 5 were waited for; matrix products, arithmetic and copies ran while one was open for 5% of the time, Pallas kernels for 0%

commit v1 on v0

v1 whole, which is shorter than its diff:
```python
import functools

import jax
import jax.numpy as jnp
from jax import lax
from jax.experimental import pallas as pl
from jax.experimental.pallas import tpu as pltpu
from jax.sharding import PartitionSpec as P

KRYLOV = 4
step_gamma = 0.4
tiny_eps = 1e-12

F32 = jnp.float32
LANES = 128
VMEM = pltpu.CompilerParams(vmem_limit_bytes=48 * 1024 * 1024)


def lane_of(rows):
    return lax.broadcasted_iota(jnp.int32, (rows, LANES), 1)


def row_of(rows):
    return lax.broadcasted_iota(jnp.int32, (rows, LANES), 0)


def roll_lanes(x, shift):
    shift %= LANES
    return pltpu.roll(x, shift, 1) if shift else x


def roll_rows(x, shift):
    return pltpu.roll(x, shift % x.shape[0], 0)


def slot_of(rows):
    return ((131 - lane_of(rows)) // 8) % 16


def two_sum(a, b):
    s = a + b
    t = s - a
    return s, (a - (s - t)) + (b - t)


def quick_sum(a, b):
    s = a + b
    return s, b - (s - a)


def split(a):
    c = a * 4097.0
    high = c - (c - a)
    return high, a - high


def two_prod(a, b):
    p = a * b
    ah, al = split(a)
    bh, bl = split(b)
    return p, ((ah * bh - p) + ah * bl + al * bh) + al * bl


def move_main(main, strip, s):
    lane = lane_of(main.shape[0])
    left = jnp.where(lane == 0, roll_lanes(strip, 8 * s + 1), roll_lanes(main, 1))
    right = jnp.where(lane == LANES - 1, roll_lanes(strip, 8 * s - 1), roll_lanes(main, -1))
    return left, right


def move_strip(mains, strip, second=None):
    rows = strip.shape[0]
    lane = lane_of(rows)
    slot = slot_of(rows)
    edge = jnp.zeros((rows, LANES), F32)
    for s, main in enumerate(mains):
        both = jnp.where(
            lane % 8 == 7, roll_lanes(main, -(8 * s + 1)), roll_lanes(main, 1 - 8 * s)
        )
        edge = jnp.where(slot == s, both, edge)
    left = jnp.where(lane % 8 == 0, edge, roll_lanes(strip, 1))
    right = jnp.where(lane % 8 == 7, edge, roll_lanes(strip, -1))
    if second is not None:
        left = jnp.where(lane % 8 == 4, roll_lanes(second, -3), left)
        right = jnp.where(lane % 8 == 3, roll_lanes(second, 3), right)
    return left, right


def drift(field, left, right, vx, vy):
    along_x = roll_rows(field, -1) - roll_rows(field, 1)
    return -0.5 * (vx * along_x + vy * (right - left))


def strip_speed(vel, count, rows):
    slot = slot_of(rows)
    vx = jnp.zeros((rows, LANES), F32)
    vy = jnp.zeros((rows, LANES), F32)
    for s in range(count):
        vx = jnp.where(slot == s, vel[s, 0], vx)
        vy = jnp.where(slot == s, vel[s, 1], vy)
    return vx, vy


def spread(strip, t):
    lane = lane_of(strip.shape[0])
    source = (LANES - 4 - 8 * t + (lane + 4) % 8) % LANES
    return jnp.take_along_axis(strip, source, axis=1)


def strip_product(get, strip, count):
    total = get(0) * spread(strip, 0)
    for t in range(1, count):
        total = total + get(t) * spread(strip, t)
    return total


def row_product(block, halo, mains, s):
    count = len(mains)
    rows = block.shape[2]
    total = block[s, 0] * mains[0][:rows]
    for t in range(1, count):
        total = total + block[s, t] * mains[t][:rows]
    if halo is None:
        return total
    extra = halo[s * count] * mains[0][rows:]
    for t in range(1, count):
        extra = extra + halo[s * count + t] * mains[t][rows:]
    return jnp.concatenate([total, extra], axis=0)


def first_vector(fields, rates, halo_rates, strips, vel, speed, store):
    state, quad, hist = fields
    count = len(state)
    state_s, quad_s, hist_s, second = strips(2 * count), strips(2 * count + 1), strips(
        2 * count + 2
    ), strips(2 * count + 3)
    for s in range(count):
        left, right = move_main(state[s], state_s, s)
        forcing = drift(state[s], left, right, vel[s, 0], vel[s, 1])
        forcing = forcing + row_product(rates, halo_rates, state, s)
        forcing = forcing - quad[s] * state[s] * state[s]
        store(s, -(state[s] - hist[s] - step_gamma * forcing))
    left, right = move_strip(state, state_s, second)
    forcing = drift(state_s, left, right, *speed)
    forcing = forcing + strip_product(strips, state_s, count)
    forcing = forcing - quad_s * state_s * state_s
    store(None, -(state_s - hist_s - step_gamma * forcing))


def apply_shifted(v, v_s, z, z_s, damp, damp_s, rates, halo_rates, strips, vel, speed, store):
    count = len(z)
    for s in range(count):
        left, right = move_main(z[s], z_s[...], s)
        jac = drift(z[s], left, right, vel[s, 0], vel[s, 1])
        jac = jac + row_product(rates, halo_rates, z, s) - damp(s) * z[s]
        store(s, (z[s] - step_gamma * jac) - v[s])
    z_s = z_s[...]
    left, right = move_strip(z, z_s)
    jac = drift(z_s, left, right, *speed)
    jac = jac + strip_product(strips, z_s, count) - damp_s * z_s
    store(None, (z_s - step_gamma * jac) - v_s)


def pack_kernel(state, history, rates, quadratic, precond, to_right, to_left):
    count, rows, _ = state.shape
    slot = slot_of(rows)
    low = lane_of(rows) % 8 < 4

    def group(index):
        packed = jnp.zeros((rows, LANES), F32)
        for s in range(count):
            if index < count:
                plane = rates[s, index]
            elif index < 2 * count:
                plane = precond[s, index - count]
            else:
                plane = (state, quadratic, history, state)[index - 2 * count][s]
            if index == 2 * count + 3:
                moved = jnp.where(
                    low, roll_lanes(plane, -4 - 8 * s), roll_lanes(plane, 4 - 8 * s)
                )
            else:
                moved = roll_lanes(plane, -8 * s)
            packed = jnp.where(slot == s, moved, packed)
        return packed

    for pair in range(count + 2):
        one, two = group(2 * pair), group(2 * pair + 1)
        to_right[pair] = jnp.where(low, roll_lanes(two, -4), one)
        to_left[pair] = jnp.where(low, one, roll_lanes(two, 4))


def half_kernel(
    from_left, from_right, state, history, rates, quadratic, precond, vel,
    strips_out, send_a, send_b, v_ref, z_ref, vs_ref, zs_ref, *, counts,
):
    count, rows, _ = state.shape
    cols, flip = counts
    low = lane_of(rows) % 8 < 4
    position = lax.axis_index("col")
    has_left = (position > 0).astype(F32)
    has_right = (position < cols - 1).astype(F32)
    for pair in range(count + 2):
        left = from_left[pair] * has_left
        right = from_right[pair] * has_right
        strips_out[2 * pair] = jnp.where(low, right, left)
        strips_out[2 * pair + 1] = jnp.where(low, roll_lanes(right, -4), roll_lanes(left, 4))

    speed = strip_speed(vel, count, rows)
    strips = lambda g: strips_out[g]
    fields = [[ref[s] for s in range(count)] for ref in (state, quadratic, history)]

    def put(k):
        def store(s, value):
            if s is None:
                vs_ref[k] = value
            else:
                v_ref[k, s] = value
        return store

    def precondition(k):
        v = [v_ref[k, s] for s in range(count)]
        for s in range(count):
            z_ref[k, s] = row_product(precond, None, v, s)
        zs_ref[k] = strip_product(lambda t: strips_out[count + t], vs_ref[k], count)

    first_vector(fields, rates, None, strips, vel, speed, put(0))
    precondition(0)
    apply_shifted(
        [v_ref[0, s] for s in range(count)], vs_ref[0],
        [z_ref[0, s] for s in range(count)], zs_ref.at[0],
        lambda s: 2.0 * quadratic[s] * state[s],
        2.0 * strips_out[2 * count + 1] * strips_out[2 * count],
        rates, None, strips, vel, speed, put(1),
    )
    precondition(1)

    odd = (lax.axis_index("parts") % 2) if flip else 0
    for target, near, far in (
        (send_a, (rows - 2) * (1 - odd), (rows - 3) * (1 - odd) + 2 * odd),
        (send_b, (rows - 2) * odd, (rows - 3) * odd + 2 * (1 - odd)),
    ):
        base = 0
        for matrix in (rates, precond):
            for s in range(count):
                for t in range(count):
                    target[base] = matrix[s, t, pl.ds(near, 2), :]
                    base += 1
        for ref in (state, quadratic, history):
            for s in range(count):
                target[base] = ref[s, pl.ds(near, 2), :]
                base += 1
        for g in range(2 * count + 4):
            target[base] = strips_out[g, pl.ds(near, 2), :]
            base += 1
        single = [state.at[s] for s in range(count)]
        single += [z_ref.at[k, s] for k in range(2) for s in range(count)]
        single += [strips_out.at[2 * count], zs_ref.at[0], zs_ref.at[1]]
        for j, ref in enumerate(single):
            target[base + j // 2, pl.ds(j % 2, 1), :] = ref[pl.ds(far, 1), :]
        if len(single) % 2:
            target[base + len(single) // 2, pl.ds(1, 1), :] = jnp.zeros((1, LANES), F32)


def message_planes(count):
    return 2 * count * count + 3 * count + (2 * count + 4) + (3 * count + 3 + 1) // 2


def pairs_of(width):
    return [(i, j) for i in range(width) for j in range(i, width)]


def full_kernel(
    got_a, got_b, strips_in, state, history, rates, quadratic, precond, vel,
    z_out, gram_out,
    halo_rates, halo_precond, fields_ref, strips_ref, inject_ref, inject_s, v_ref, vs_ref,
    zx_ref, zs_ref, *, row_count, flip,
):
    count, rows, _ = state.shape
    ext = rows + 8
    odd = (lax.axis_index("parts") % 2) if flip else 0
    position = lax.axis_index("row")
    above = (position > 0).astype(F32)
    below = (position < row_count - 1).astype(F32)
    odd_f = jnp.asarray(odd).astype(F32)
    keep_a = above * (1 - odd_f) + below * odd_f
    keep_b = below * (1 - odd_f) + above * odd_f
    near_a, far_a = 6 * (1 - odd), 5 * (1 - odd) + 2 * odd
    near_b, far_b = 6 * odd, 5 * odd + 2 * (1 - odd)
    sources = ((got_a, keep_a, near_a, far_a), (got_b, keep_b, near_b, far_b))
    blank = jnp.zeros((8, LANES), F32)

    def receive(target, base, at=0):
        target[pl.ds(at, 8), :] = blank
        for source, keep, near, _ in sources:
            target[pl.ds(at + near, 2), :] = source[base] * keep

    base = 0
    for halo in (halo_rates, halo_precond):
        for k in range(count * count):
            receive(halo.at[k], base)
            base += 1
    for f, ref in enumerate((state, quadratic, history)):
        for s in range(count):
            fields_ref[f, s, 0:rows, :] = ref[s]
            receive(fields_ref.at[f, s], base, rows)
            base += 1
    for g in range(2 * count + 4):
        strips_ref[g, 0:rows, :] = strips_in[g]
        receive(strips_ref.at[g], base, rows)
        base += 1
    single = [(fields_ref.at[0, s], rows) for s in range(count)]
    for k in range(2):
        for s in range(count):
            inject_ref[k, s] = blank
            single.append((inject_ref.at[k, s], 0))
    single.append((strips_ref.at[2 * count], rows))
    for k in range(2):
        inject_s[k] = blank
        single.append((inject_s.at[k], 0))
    for j, (target, at) in enumerate(single):
        for source, keep, _, far in sources:
            target[pl.ds(at + far, 1), :] = source[base + j // 2, pl.ds(j % 2, 1), :] * keep

    speed = strip_speed(vel, count, ext)
    strips = lambda g: strips_ref[g]

    def put(k):
        def store(s, value):
            if s is None:
                vs_ref[k] = value
            else:
                v_ref[k, s] = value
        return store

    fields = [[fields_ref[f, s] for s in range(count)] for f in range(3)]
    first_vector(fields, rates, halo_rates, strips, vel, speed, put(0))

    far_row = (row_of(8) == 2) | (row_of(8) == 5)

    def patch(value, inject):
        return jnp.concatenate(
            [value[:rows], jnp.where(far_row, inject, value[rows:])], axis=0
        )

    for k in range(KRYLOV):
        pick = min(k, 1)
        v = [v_ref[k, s] for s in range(count)]
        for s in range(count):
            value = patch(row_product(precond, halo_precond, v, s), inject_ref[pick, s])
            zx_ref[s] = value
            z_out[k, s] = value[:rows]
        v_s = vs_ref[k]
        z_s = strip_product(lambda t: strips_ref[count + t], v_s, count)
        zs_ref[...] = patch(z_s, inject_s[pick])
        z = [zx_ref[s] for s in range(count)]
        apply_shifted(
            v, v_s, z, zs_ref,
            lambda s: 2.0 * fields_ref[1, s] * fields_ref[0, s],
            2.0 * strips_ref[2 * count + 1] * strips_ref[2 * count],
            rates, halo_rates, strips, vel, speed, put(k + 1),
        )

    pairs = pairs_of(KRYLOV + 1)

    def gather(s, carry):
        high, low = list(carry[0]), list(carry[1])
        for r in range(0, rows, 8):
            whole = [v_ref[k, s, r : r + 8, :] for k in range(KRYLOV + 1)]
            parts = [split(x) for x in whole]
            for n, (i, j) in enumerate(pairs):
                product = parts[i][0] * parts[j][0]
                rest = parts[i][0] * parts[j][1] + parts[i][1] * whole[j]
                high[n], error = two_sum(high[n], product)
                low[n] = low[n] + (error + rest)
        return tuple(high), tuple(low)

    zeros = tuple(blank for _ in pairs)
    high, low = lax.fori_loop(0, count, gather, (zeros, zeros))

    def fold(h, l, shift, move):
        h, error = two_sum(h, move(h, shift))
        return h, l + move(l, shift) + error

    row16, lane16 = row_of(16), lane_of(16)
    top = jnp.zeros((16, LANES), F32)
    bottom = jnp.zeros((16, LANES), F32)
    for n in range(len(pairs)):
        h, l = high[n], low[n]
        for shift in (4, 2, 1):
            h, l = fold(h, l, shift, roll_rows)
        top = jnp.where(row16 == n, jnp.concatenate([h, h], axis=0), top)
        bottom = jnp.where(row16 == n, jnp.concatenate([l, l], axis=0), bottom)
    for shift in (64, 32, 16, 8, 4, 2, 1):
        top, bottom = fold(top, bottom, shift, roll_lanes)
    top, bottom = quick_sum(top, bottom)
    bottom = roll_lanes(bottom, 16)
    line = jnp.where(row16 == lane16, top, 0.0) + jnp.where(row16 + 16 == lane16, bottom, 0.0)
    line = line[:8] + line[8:]
    for shift in (4, 2, 1):
        line = line + roll_rows(line, shift)
    for r in range(0, gram_out.shape[0], 8):
        gram_out[r : r + 8, :] = line


def small_problem(gram):
    width = KRYLOV + 1
    work = dict(gram)
    unit = {}
    pivot = []
    for k in range(width):
        dh, dl = work[k, k]
        pivot.append(jnp.maximum(dh, 0.0))
        inverse = jnp.where(dh > 0.0, 1.0 / jnp.where(dh > 0.0, dh, 1.0), 0.0)
        factor = {}
        for i in range(k + 1, width):
            sh, sl = work[k, i]
            q = sh * inverse
            p, e = two_prod(q, dh)
            rest = ((sh - p) - e) + (sl - q * dl)
            factor[i] = quick_sum(q, rest * inverse)
            unit[k, i] = factor[i][0]
        for i in range(k + 1, width):
            for j in range(i, width):
                fh, fl = factor[i]
                sh, sl = work[k, j]
                p, e = two_prod(fh, sh)
                e = e + (fh * sl + fl * sh)
                wh, wl = work[i, j]
                h, error = two_sum(wh, -p)
                work[i, j] = quick_sum(h, error + (wl - e))
    norm = [jnp.sqrt(d) for d in pivot]
    back = [jnp.where(n > 0.0, 1.0 / jnp.where(n > 0.0, n, 1.0), 0.0) for n in norm]
    inv = {}
    for j in range(KRYLOV):
        column = {j: None}
        inv[j, j] = back[j]
        for i in reversed(range(j)):
            total = unit[i, j] * back[j]
            for m in range(i + 1, j):
                total = total + unit[i, m] * inv[m, j]
            inv[i, j] = -total
    arnoldi = {}
    for j in range(KRYLOV):
        shifted = [inv[0, j]]
        for i in range(1, j + 1):
            shifted.append(inv[i, j] + inv[i - 1, j])
        shifted.append(inv[j, j])
        for i in range(j + 2):
            total = shifted[i]
            for m in range(i + 1, j + 2):
                total = total + unit[i, m] * shifted[m]
            arnoldi[i, j] = norm[i] * total
    beta = jnp.sqrt(pivot[0] + tiny_eps)
    basis = [[norm[0] / beta]]
    hessen = {}
    for k in range(KRYLOV):
        vector = []
        for i in range(k + 2):
            terms = [arnoldi[i, j] * basis[k][j] for j in range(max(i - 1, 0), k + 1)]
            vector.append(functools.reduce(jnp.add, terms))
        for i in range(k + 1):
            terms = [a * b for a, b in zip(basis[i], vector)]
            hessen[i, k] = functools.reduce(jnp.add, terms)
        for m in range(k + 1):
            terms = [hessen[i, k] * basis[i][m] for i in range(m, k + 1)]
            vector[m] = vector[m] - functools.reduce(jnp.add, terms)
        squared = functools.reduce(jnp.add, [x * x for x in vector])
        size = jnp.sqrt(squared + tiny_eps)
        hessen[k + 1, k] = size
        basis.append([x / size for x in vector])
    rotated = [beta] + [jnp.zeros_like(beta)] * KRYLOV
    for k in range(KRYLOV):
        first, second = hessen[k, k], hessen[k + 1, k]
        radius = jnp.sqrt(first * first + second * second)
        cosine, sine = first / radius, second / radius
        for j in range(k, KRYLOV):
            upper = hessen[k, j]
            under = hessen.get((k + 1, j))
            hessen[k, j] = cosine * upper + sine * under
            hessen[k + 1, j] = cosine * under - sine * upper
        rotated[k], rotated[k + 1] = (
            cosine * rotated[k] + sine * rotated[k + 1],
            cosine * rotated[k + 1] - sine * rotated[k],
        )
    coef = [None] * KRYLOV
    for k in reversed(range(KRYLOV)):
        total = rotated[k]
        for j in range(k + 1, KRYLOV):
            total = total - hessen[k, j] * coef[j]
        coef[k] = total / hessen[k, k]
    in_q = [
        functools.reduce(jnp.add, [coef[k] * basis[k][m] for k in range(m, KRYLOV)])
        for m in range(KRYLOV)
    ]
    in_v = [
        functools.reduce(jnp.add, [inv[i, j] * in_q[j] for j in range(i, KRYLOV)])
        for i in range(KRYLOV)
    ]
    return in_v, jnp.abs(rotated[KRYLOV])


def solve_kernel(gathered, z_ref, state, updated, residual):
    count, rows, _ = state.shape
    high = gathered[0:8, :]
    low = roll_lanes(high, -16)
    for r in range(8, gathered.shape[0], 8):
        tile = gathered[r : r + 8, :]
        high, error = two_sum(high, tile)
        low = low + roll_lanes(tile, -16) + error
    for shift in (4, 2, 1):
        high, error = two_sum(high, roll_rows(high, shift))
        low = low + roll_rows(low, shift) + error
    high, low = quick_sum(high, low)
    gram = {}
    for n, pair in enumerate(pairs_of(KRYLOV + 1)):
        gram[pair] = (
            jnp.broadcast_to(high[:, n : n + 1], (8, LANES)),
            jnp.broadcast_to(low[:, n : n + 1], (8, LANES)),
        )
    weights, last = small_problem(gram)
    for s in range(count):
        for r in range(0, rows, 8):
            total = weights[0] * z_ref[0, s, r : r + 8, :]
            for k in range(1, KRYLOV):
                total = total + weights[k] * z_ref[k, s, r : r + 8, :]
            updated[s, r : r + 8, :] = state[s, r : r + 8, :] + total
    residual[:, :] = last


def shapes(*dims):
    return jax.ShapeDtypeStruct(dims, F32)


def body(state, history, rates, quadratic, velocity, precond):
    count, rows, _ = state.shape
    part_count = lax.axis_size("parts")
    row_count = lax.axis_size("row")
    col_count = lax.axis_size("col")
    flip = part_count % 2 == 0
    block = (count, rows, LANES)

    to_right, to_left = pl.pallas_call(
        pack_kernel,
        out_shape=[shapes(count + 2, rows, LANES)] * 2,
        compiler_params=VMEM,
        name="pack_columns",
    )(state, history, rates, quadratic, precond)
    ring = [(i, (i + 1) % col_count) for i in range(col_count)]
    from_left = lax.ppermute(to_right, "col", ring)
    from_right = lax.ppermute(to_left, "col", [(b, a) for a, b in ring])

    smem = pl.BlockSpec(memory_space=pltpu.SMEM)
    whole = pl.BlockSpec(memory_space=pltpu.VMEM)
    planes = message_planes(count)
    strips, send_a, send_b = pl.pallas_call(
        functools.partial(half_kernel, counts=(col_count, flip)),
        in_specs=[whole] * 7 + [smem],
        out_shape=[shapes(2 * count + 4, rows, LANES)] + [shapes(planes, 2, LANES)] * 2,
        scratch_shapes=[
            pltpu.VMEM((2,) + block, F32),
            pltpu.VMEM((2,) + block, F32),
            pltpu.VMEM((2, rows, LANES), F32),
            pltpu.VMEM((2, rows, LANES), F32),
        ],
        compiler_params=VMEM,
        name="half_step",
    )(from_left, from_right, state, history, rates, quadratic, precond, velocity)

    chain = []
    for p in range(part_count):
        for r in range(row_count):
            if flip and p % 2:
                target = (p, r - 1) if r else (p - 1, 0)
            elif flip:
                target = (p, r + 1) if r < row_count - 1 else (p + 1, r)
            else:
                target = (p, (r + 1) % row_count)
            chain.append((p * row_count + r, target[0] * row_count + target[1]))
    got_a = lax.ppermute(send_a, ("parts", "row"), chain)
    got_b = lax.ppermute(send_b, ("parts", "row"), [(b, a) for a, b in chain])

    ext = rows + 8
    members = row_count * col_count
    z, gram = pl.pallas_call(
        functools.partial(full_kernel, row_count=row_count, flip=flip),
        in_specs=[whole] * 8 + [smem],
        out_shape=[shapes(KRYLOV, *block), shapes(members, LANES)],
        scratch_shapes=[
            pltpu.VMEM((count * count, 8, LANES), F32),
            pltpu.VMEM((count * count, 8, LANES), F32),
            pltpu.VMEM((3, count, ext, LANES), F32),
            pltpu.VMEM((2 * count + 4, ext, LANES), F32),
            pltpu.VMEM((2, count, 8, LANES), F32),
            pltpu.VMEM((2, 8, LANES), F32),
            pltpu.VMEM((KRYLOV + 1, count, ext, LANES), F32),
            pltpu.VMEM((KRYLOV + 1, ext, LANES), F32),
            pltpu.VMEM((count, ext, LANES), F32),
            pltpu.VMEM((ext, LANES), F32),
        ],
        compiler_params=VMEM,
        name="krylov",
    )(got_a, got_b, strips, state, history, rates, quadratic, precond, velocity)

    gathered = lax.all_to_all(gram, ("row", "col"), 0, 0, tiled=True)
    updated, last = pl.pallas_call(
        solve_kernel,
        out_shape=[shapes(*block), shapes(8, LANES)],
        compiler_params=VMEM,
        name="solve",
    )(gathered, z, state)
    return updated, last[0, :1]


def solution(mesh):
    placed = (
        P(None, ("parts", "row"), "col"),
        P(None, ("parts", "row"), "col"),
        P(None, None, ("parts", "row"), "col"),
        P(None, ("parts", "row"), "col"),
        P(),
        P(None, None, ("parts", "row"), "col"),
    )
    return jax.shard_map(
        body,
        mesh=mesh,
        in_specs=placed,
        out_specs=(P(None, ("parts", "row"), "col"), P("parts")),
        check_vma=False,
    )
```

time: 281 us -> 43.3 us (0.15)
  blocking collectives: 156 us -> 11.9 us
  starting transfers between devices: 52 us -> 4.6 us
  between operations: 33.8 us -> 0.69 us
  other arithmetic: 19.4 us -> 0 us
  local copies, waits for them, and re-layouts: 15 us -> 5.57 us
  waiting for transfers between devices: 3.3 us -> 11.8 us
  Pallas kernels: 0 us -> 8.41 us
    psum x5 -> x0, blocking collectives: 156 us -> none  [the longest x4 123 us: body(): lax.psum((local_dots, jnp.sum(vector * vector)), ('row', 'col'))]
    ppermute x20 -> x4, starting transfers between devices: 52 us -> 4.6 us  [the longest x1 1.98 us: body(): from_right = lax.ppermute(to_left, 'col', [(b, a) for a, b in ring])]
    all_to_all x0 -> x1, blocking collectives: none -> 11.9 us  [body(): gathered = lax.all_to_all(gram, ('row', 'col'), 0, 0, tiled=True)]
    reduce_sum x26 -> x0, other arithmetic: 9.8 us -> none  [the longest x3 2.36 us: body(): jnp.sum(vector * vector)]
    ppermute x20 -> x4, waiting for transfers between devices: 3.3 us -> 11.8 us  [the longest x1 6.9 us: body(): got_a = lax.ppermute(send_a, ('parts', 'row'), chain)]
    pallas_call x0 -> x4, Pallas kernels: none -> 8.41 us  [the longest x1 4.43 us: body(): pl.pallas_call(functools.partial(full_kernel, row_count=row_count, flip=f...]
    another operation x9 -> x0, other arithmetic: 7.83 us -> none
    slice x23 -> x1, local copies, waits for them, and re-layouts: 7.73 us -> 0.51 us  [body(): return (updated, last[0, :1])]
  transfers between devices with their start and end apart: 20 -> 4, of which waited for: 5 -> 4; matrix products, arithmetic and copies ran while one was open for 5% -> 0% of each run, Pallas kernels for 0% -> 0%
where the time goes in v1:
time: 43.3 us; the launch traced here: 43 us
  blocking collectives  11.9 us (27%)
  waiting for transfers between devices  11.8 us (27%)
  Pallas kernels  8.41 us (19%)
  local copies, waits for them, and re-layouts  5.57 us (13%)
  starting transfers between devices  4.6 us (11%)
  between operations  0.69 us (2%)
    all_to_all x1, blocking collectives, body(): gathered = lax.all_to_all(gram, ('row', 'col'), 0, 0, tiled=True)  11.9 us
    ppermute x1, waiting for transfers between devices, body(): got_a = lax.ppermute(send_a, ('parts', 'row'), chain)  6.9 us
    unnamed x23, local copies, waits for them, and re-layouts  5.06 us
    pallas_call x1, Pallas kernels, body(): pl.pallas_call(functools.partial(full_kernel, row_count=row_count, flip=f...  4.43 us
    ppermute x1, waiting for transfers between devices, body(): from_left = lax.ppermute(to_right, 'col', ring)  2.14 us
    ppermute x1, starting transfers between devices, body(): from_right = lax.ppermute(to_left, 'col', [(b, a) for a, b in ring])  1.98 us
    ppermute x1, waiting for transfers between devices, body(): got_b = lax.ppermute(send_b, ('parts', 'row'), [(b, a) for a, b in chain])  1.86 us
    pallas_call x1, Pallas kernels, body(): pl.pallas_call(functools.partial(half_kernel, counts=(col_count, flip)),...  1.66 us
  transfers between devices with their start and end apart: 4, of which 4 were waited for; matrix products, arithmetic and copies ran while one was open for 0% of the time, Pallas kernels for 0%

profile of v1, /device:TPU:0, one launch (start us, length us, event | category | flops | bytes accessed | tf_op | source)
XLA Modules:
  0.0 43.0 jit_solution(14854549077564462920)
XLA Ops:
  0.6 0.0 copy-start
  0.6 1.1 %copy-done = f32[10,10,16,128]{3,2,1,0:T(8,128)S(1)} copy-done((f32[10,10,16,128]{3,2,1,0:T(8,128)S(1)}, f32[10,10,16,128]{3,2,1,0:T(8,128)}, u32[]{:S(2)}) %copy-start) | copy-done | bytes 819224
  1.8 0.0 copy-start.2
  1.8 1.1 %copy-done.2 = f32[10,10,16,128]{3,2,1,0:T(8,128)S(1)} copy-done((f32[10,10,16,128]{3,2,1,0:T(8,128)S(1)}, f32[10,10,16,128]{3,2,1,0:T(8,128)}, u32[]{:S(2)}) %copy-start.2) | copy-done | bytes 819224
  2.9 0.0 copy-start.4
  2.9 0.9 %copy-done.4 = f32[10,16,128]{2,1,0:T(8,128)S(1)} copy-done((f32[10,16,128]{2,1,0:T(8,128)S(1)}, f32[10,16,128]{2,1,0:T(8,128)}, u32[]{:S(2)}) %copy-start.4) | copy-done | bytes 81944
  3.8 0.0 copy-start.6
  3.8 0.9 %copy-done.6 = f32[10,16,128]{2,1,0:T(8,128)S(1)} copy-done((f32[10,16,128]{2,1,0:T(8,128)S(1)}, f32[10,16,128]{2,1,0:T(8,128)}, u32[]{:S(2)}) %copy-start.6) | copy-done | bytes 81944
  4.7 0.0 copy-start.8
  4.7 0.9 %copy-done.8 = f32[10,16,128]{2,1,0:T(8,128)S(1)} copy-done((f32[10,16,128]{2,1,0:T(8,128)S(1)}, f32[10,16,128]{2,1,0:T(8,128)}, u32[]{:S(2)}) %copy-start.8) | copy-done | bytes 81944
  5.6 0.0 copy-start.1
  5.6 0.0 copy-start.3
  5.6 0.0 copy-start.5
  5.6 0.0 copy-start.7
  5.6 0.0 copy-start.9
  5.6 1.3 %pack_columns.1 = (f32[12,16,128]{2,1,0:T(8,128)S(1)}, f32[12,16,128]{2,1,0:T(8,128)S(1)}) custom-call(f32[10,16,128]{2,1,0:T(8,128)S(1)} %copy-done.4, f32[10,16,128]{2,1,0:T(8,128)S(1)} %copy-done.6, f32[10,10,16,128]{3,2,1,0:T(8,128)S(1)} %copy-done, f32[10,16,128]{2,1,0:T(8,128)S(1)} %copy-done.8, f32[10,10,16,128]{3,2,1,0:T(8,128)S(1)} %copy-done.2), custom_call_target="tpu_custom_call" | custom-call | tf_op jit(solution)/shard_map/pack_columns/pallas_call | solution.py:543
  6.9 0.0 copy-start.10
  6.9 0.5 %collective-permute-start = (f32[12,16,128]{2,1,0:T(8,128)S(1)}, f32[12,16,128]{2,1,0:T(8,128)S(1)}, u32[]{:S(2)}, u32[]{:S(2)}) collective-permute-start(f32[12,16,128]{2,1,0:T(8,128)S(1)} %get-tuple-element.11), channel_id=1, source_target_pairs={{0,1},{1,2},{2,3},{3,0},{4,5},{5,6},{6,7},{7,4},{8,9},{9,10},{10,1... | collective-permute-start | bytes 294920 | tf_op jit(solution)/shard_map/ppermute | solution.py:550
  7.4 2.0 %collective-permute-start.1 = (f32[12,16,128]{2,1,0:T(8,128)S(1)}, f32[12,16,128]{2,1,0:T(8,128)S(1)}, u32[]{:S(2)}, u32[]{:S(2)}) collective-permute-start(f32[12,16,128]{2,1,0:T(8,128)S(1)} %get-tuple-element.12), channel_id=1, source_target_pairs={{1,0},{2,1},{3,2},{0,3},{5,4},{6,5},{7,6},{4,7},{9,8},{10,9},{11,1... | collective-permute-start | bytes 294920 | tf_op jit(solution)/shard_map/ppermute | solution.py:551
  9.4 0.0 copy-done.10
  9.4 0.1 copy.10.vel
  9.5 2.1 %collective-permute-done.from_left = f32[12,16,128]{2,1,0:T(8,128)S(1)} collective-permute-done((f32[12,16,128]{2,1,0:T(8,128)S(1)}, f32[12,16,128]{2,1,0:T(8,128)S(1)}, u32[]{:S(2)}, u32[]{:S(2)}) %collective-permute-start) | collective-permute-done | bytes 98336 | tf_op jit(solution)/shard_map/ppermute | solution.py:550
  11.6 0.9 %collective-permute-done.1.from_right = f32[12,16,128]{2,1,0:T(8,128)S(1)} collective-permute-done((f32[12,16,128]{2,1,0:T(8,128)S(1)}, f32[12,16,128]{2,1,0:T(8,128)S(1)}, u32[]{:S(2)}, u32[]{:S(2)}) %collective-permute-start.1) | collective-permute-done | bytes 98336 | tf_op jit(solution)/shard_map/ppermute | solution.py:551
  12.5 0.0 copy-done.1
  12.5 0.0 copy-done.3
  12.5 0.0 copy-done.5
  12.5 0.0 copy-done.7
  12.5 0.0 copy-done.9
  12.5 1.7 %half_step.1 = (f32[24,16,128]{2,1,0:T(8,128)S(1)}, f32[271,2,128]{2,1,0:T(2,128)S(1)}, f32[271,2,128]{2,1,0:T(2,128)S(1)}) custom-call(f32[12,16,128]{2,1,0:T(8,128)S(1)} %collective-permute-done.from_left, f32[12,16,128]{2,1,0:T(8,128)S(1)} %collective-permute-done.1.from_right, f32[10,16,128]{2,1,0:T(8,128)S(1)} %copy-done.5, ...), custom_call_target="tpu_custom_call" | custom-call | tf_op jit(solution)/shard_map/half_step/pallas_call | solution.py:556
  14.2 1.6 %collective-permute-start.2 = (f32[271,2,128]{2,1,0:T(2,128)S(1)}, f32[271,2,128]{2,1,0:T(2,128)S(1)}, u32[]{:S(2)}, u32[]{:S(2)}) collective-permute-start(f32[271,2,128]{2,1,0:T(2,128)S(1)} %get-tuple-element.13), channel_id=1, source_target_pairs={{0,4},{4,8},{8,12},{12,28},{16,0},{20,16},{24,20},{28,24},{1,5},{5... | collective-permute-start | bytes 832520 | tf_op jit(solution)/shard_map/ppermute | solution.py:580
  15.8 0.4 %collective-permute-start.3 = (f32[271,2,128]{2,1,0:T(2,128)S(1)}, f32[271,2,128]{2,1,0:T(2,128)S(1)}, u32[]{:S(2)}, u32[]{:S(2)}) collective-permute-start(f32[271,2,128]{2,1,0:T(2,128)S(1)} %get-tuple-element.14), channel_id=1, source_target_pairs={{4,0},{8,4},{12,8},{28,12},{0,16},{16,20},{20,24},{24,28},{5,1},{9... | collective-permute-start | bytes 832520 | tf_op jit(solution)/shard_map/ppermute | solution.py:581
  16.3 6.9 %collective-permute-done.2.got_a = f32[271,2,128]{2,1,0:T(2,128)S(1)} collective-permute-done((f32[271,2,128]{2,1,0:T(2,128)S(1)}, f32[271,2,128]{2,1,0:T(2,128)S(1)}, u32[]{:S(2)}, u32[]{:S(2)}) %collective-permute-start.2) | collective-permute-done | bytes 277536 | tf_op jit(solution)/shard_map/ppermute | solution.py:580
  23.2 1.9 %collective-permute-done.3.got_b = f32[271,2,128]{2,1,0:T(2,128)S(1)} collective-permute-done((f32[271,2,128]{2,1,0:T(2,128)S(1)}, f32[271,2,128]{2,1,0:T(2,128)S(1)}, u32[]{:S(2)}, u32[]{:S(2)}) %collective-permute-start.3) | collective-permute-done | bytes 277536 | tf_op jit(solution)/shard_map/ppermute | solution.py:581
  25.0 4.4 %krylov.1 = (f32[4,10,16,128]{3,2,1,0:T(8,128)S(1)}, f32[16,128]{1,0:T(8,128)S(1)}) custom-call(f32[271,2,128]{2,1,0:T(2,128)S(1)} %collective-permute-done.2.got_a, f32[271,2,128]{2,1,0:T(2,128)S(1)} %collective-permute-done.3.got_b, f32[24,16,128]{2,1,0:T(8,128)S(1)} %get-tuple-element.15.strips_in, f32[10,16,128]{2,1,0:T(8,128)S(1)} %copy-done.5, ...), custom_call_target="tpu_custom_call" | custom-call | tf_op jit(solution)/shard_map/krylov/pallas_call | solution.py:585
  29.5 11.9 %all_to_all.11 = f32[16,1,128]{2,1,0:T(1,128)S(1)} all-to-all(f32[16,1,128]{2,1,0:T(1,128)S(1)} %bitcast.6), channel_id=1, replica_groups=mesh['parts'=2,'row'=4,'col'=4] {'row','col'}, dimensions={0} | all-to-all | bytes 16384 | tf_op jit(solution)/shard_map/all_to_all | solution.py:605
  41.4 1.1 %solve.1 = (f32[10,16,128]{2,1,0:T(8,128)}, f32[8,128]{1,0:T(8,128)S(1)}) custom-call(f32[16,128]{1,0:T(8,128)S(1)} %bitcast.5, f32[4,10,16,128]{3,2,1,0:T(8,128)S(1)} %get-tuple-element.17.z_ref, f32[10,16,128]{2,1,0:T(8,128)S(1)} %copy-done.5), custom_call_target="tpu_custom_call" | custom-call | tf_op jit(solution)/shard_map/solve/pallas_call | solution.py:606
  42.5 0.5 %slice.3 = f32[1,1]{1,0:T(1,128)} slice(f32[8,128]{1,0:T(8,128)S(1)} %get-tuple-element.19), slice={[0:1], [0:1]} | slice | bytes 8 | tf_op jit(solution)/shard_map/slice | solution.py:612
Async XLA Ops:
  0.6 1.1 %copy-start = (f32[10,10,16,128]{3,2,1,0:T(8,128)S(1)}, f32[10,10,16,128]{3,2,1,0:T(8,128)}, u32[]{:S(2)}) copy-start(f32[10,10,16,128]{3,2,1,0:T(8,128)} %rates.5) | copy-start | bytes 2457604
  1.8 1.1 %copy-start.2 = (f32[10,10,16,128]{3,2,1,0:T(8,128)S(1)}, f32[10,10,16,128]{3,2,1,0:T(8,128)}, u32[]{:S(2)}) copy-start(f32[10,10,16,128]{3,2,1,0:T(8,128)} %precond.5) | copy-start | bytes 2457604
  2.9 0.9 %copy-start.4 = (f32[10,16,128]{2,1,0:T(8,128)S(1)}, f32[10,16,128]{2,1,0:T(8,128)}, u32[]{:S(2)}) copy-start(f32[10,16,128]{2,1,0:T(8,128)} %state.7) | copy-start | bytes 245764
  3.8 0.9 %copy-start.6 = (f32[10,16,128]{2,1,0:T(8,128)S(1)}, f32[10,16,128]{2,1,0:T(8,128)}, u32[]{:S(2)}) copy-start(f32[10,16,128]{2,1,0:T(8,128)} %history.5) | copy-start | bytes 245764
  4.7 0.9 %copy-start.8 = (f32[10,16,128]{2,1,0:T(8,128)S(1)}, f32[10,16,128]{2,1,0:T(8,128)}, u32[]{:S(2)}) copy-start(f32[10,16,128]{2,1,0:T(8,128)} %quadratic.5) | copy-start | bytes 245764
  5.6 6.9 %copy-start.1 = (f32[10,10,16,128]{3,2,1,0:T(8,128)S(1)}, f32[10,10,16,128]{3,2,1,0:T(8,128)}, u32[]{:S(2)}) copy-start(f32[10,10,16,128]{3,2,1,0:T(8,128)} %rates.5) | copy-start | bytes 2457604
  5.6 6.9 %copy-start.3 = (f32[10,10,16,128]{3,2,1,0:T(8,128)S(1)}, f32[10,10,16,128]{3,2,1,0:T(8,128)}, u32[]{:S(2)}) copy-start(f32[10,10,16,128]{3,2,1,0:T(8,128)} %precond.5) | copy-start | bytes 2457604
  5.6 6.9 %copy-start.5 = (f32[10,16,128]{2,1,0:T(8,128)S(1)}, f32[10,16,128]{2,1,0:T(8,128)}, u32[]{:S(2)}) copy-start(f32[10,16,128]{2,1,0:T(8,128)} %state.7) | copy-start | bytes 245764
  5.6 6.9 %copy-start.7 = (f32[10,16,128]{2,1,0:T(8,128)S(1)}, f32[10,16,128]{2,1,0:T(8,128)}, u32[]{:S(2)}) copy-start(f32[10,16,128]{2,1,0:T(8,128)} %history.5) | copy-start | bytes 245764
  5.6 6.9 %copy-start.9 = (f32[10,16,128]{2,1,0:T(8,128)S(1)}, f32[10,16,128]{2,1,0:T(8,128)}, u32[]{:S(2)}) copy-start(f32[10,16,128]{2,1,0:T(8,128)} %quadratic.5) | copy-start | bytes 245764
  6.9 2.5 %copy-start.10 = (f32[10,2]{0,1:T(2,128)S(1)}, f32[10,2]{0,1:T(2,128)}, u32[]{:S(2)}) copy-start(f32[10,2]{0,1:T(2,128)} %param.10) | copy-start | bytes 244
  6.9 4.8 %collective-permute-start = (f32[12,16,128]{2,1,0:T(8,128)S(1)}, f32[12,16,128]{2,1,0:T(8,128)S(1)}, u32[]{:S(2)}, u32[]{:S(2)}) collective-permute-start(f32[12,16,128]{2,1,0:T(8,128)S(1)} %get-tuple-element.11), channel_id=1, source_target_pairs={{0,1},{1,2},{2,3},{3,0},{4,5},{5,6},{6,7},{7,4},{8,9},{9,10},{10,1... | collective-permute-start | bytes 294920 | tf_op jit(solution)/shard_map/ppermute | solution.py:550
  7.4 5.1 %collective-permute-start.1 = (f32[12,16,128]{2,1,0:T(8,128)S(1)}, f32[12,16,128]{2,1,0:T(8,128)S(1)}, u32[]{:S(2)}, u32[]{:S(2)}) collective-permute-start(f32[12,16,128]{2,1,0:T(8,128)S(1)} %get-tuple-element.12), channel_id=1, source_target_pairs={{1,0},{2,1},{3,2},{0,3},{5,4},{6,5},{7,6},{4,7},{9,8},{10,9},{11,1... | collective-permute-start | bytes 294920 | tf_op jit(solution)/shard_map/ppermute | solution.py:551
  14.2 9.0 %collective-permute-start.2 = (f32[271,2,128]{2,1,0:T(2,128)S(1)}, f32[271,2,128]{2,1,0:T(2,128)S(1)}, u32[]{:S(2)}, u32[]{:S(2)}) collective-permute-start(f32[271,2,128]{2,1,0:T(2,128)S(1)} %get-tuple-element.13), channel_id=1, source_target_pairs={{0,4},{4,8},{8,12},{12,28},{16,0},{20,16},{24,20},{28,24},{1,5},{5... | collective-permute-start | bytes 832520 | tf_op jit(solution)/shard_map/ppermute | solution.py:580
  15.8 9.2 %collective-permute-start.3 = (f32[271,2,128]{2,1,0:T(2,128)S(1)}, f32[271,2,128]{2,1,0:T(2,128)S(1)}, u32[]{:S(2)}, u32[]{:S(2)}) collective-permute-start(f32[271,2,128]{2,1,0:T(2,128)S(1)} %get-tuple-element.14), channel_id=1, source_target_pairs={{4,0},{8,4},{12,8},{28,12},{0,16},{16,20},{20,24},{24,28},{5,1},{9... | collective-permute-start | bytes 832520 | tf_op jit(solution)/shard_map/ppermute | solution.py:581

commit v2 on v1

--- a/solution.py
+++ b/solution.py
@@ -161,8 +161,25 @@
     store(None, (z_s - step_gamma * jac) - v_s)
 
 
-def pack_kernel(state, history, rates, quadratic, precond, to_right, to_left):
+def pack_kernel(
+    state_in, history_in, rates_in, quadratic_in, precond_in,
+    state, history, rates, quadratic, precond, to_right, to_left, sems,
+):
     count, rows, _ = state.shape
+    copies = [
+        pltpu.make_async_copy(source, target, sems.at[n])
+        for n, (source, target) in enumerate(
+            (
+                (rates_in, rates),
+                (precond_in, precond),
+                (state_in, state),
+                (quadratic_in, quadratic),
+                (history_in, history),
+            )
+        )
+    ]
+    for copy in copies:
+        copy.start()
     slot = slot_of(rows)
     low = lane_of(rows) % 8 < 4
 
@@ -184,7 +201,13 @@
             packed = jnp.where(slot == s, moved, packed)
         return packed
 
+    done = set()
     for pair in range(count + 2):
+        ready = 1 if 2 * pair + 1 < count else 2 if 2 * pair + 1 < 2 * count else 5
+        for n in range(ready):
+            if n not in done:
+                copies[n].wait()
+                done.add(n)
         one, two = group(2 * pair), group(2 * pair + 1)
         to_right[pair] = jnp.where(low, roll_lanes(two, -4), one)
         to_left[pair] = jnp.where(low, one, roll_lanes(two, 4))
@@ -525,7 +548,7 @@
             for k in range(1, KRYLOV):
                 total = total + weights[k] * z_ref[k, s, r : r + 8, :]
             updated[s, r : r + 8, :] = state[s, r : r + 8, :] + total
-    residual[:, :] = last
+    residual[0] = last[0, 0]
 
 
 def shapes(*dims):
@@ -540,18 +563,29 @@
     flip = part_count % 2 == 0
     block = (count, rows, LANES)
 
-    to_right, to_left = pl.pallas_call(
+    square = (count,) + block
+    smem = pl.BlockSpec(memory_space=pltpu.SMEM)
+    whole = pl.BlockSpec(memory_space=pltpu.VMEM)
+    inputs = [
+        pltpu.with_memory_space_constraint(x, pltpu.HBM)
+        for x in (state, history, rates, quadratic, precond)
+    ]
+    state, history, rates, quadratic, precond, to_right, to_left = pl.pallas_call(
         pack_kernel,
-        out_shape=[shapes(count + 2, rows, LANES)] * 2,
+        in_specs=[pl.BlockSpec(memory_space=pltpu.HBM)] * 5,
+        out_shape=[
+            shapes(*block), shapes(*block), shapes(*square), shapes(*block), shapes(*square),
+            shapes(count + 2, rows, LANES), shapes(count + 2, rows, LANES),
+        ],
+        out_specs=[whole] * 7,
+        scratch_shapes=[pltpu.SemaphoreType.DMA((5,))],
         compiler_params=VMEM,
         name="pack_columns",
-    )(state, history, rates, quadratic, precond)
+    )(*inputs)
     ring = [(i, (i + 1) % col_count) for i in range(col_count)]
     from_left = lax.ppermute(to_right, "col", ring)
     from_right = lax.ppermute(to_left, "col", [(b, a) for a, b in ring])
 
-    smem = pl.BlockSpec(memory_space=pltpu.SMEM)
-    whole = pl.BlockSpec(memory_space=pltpu.VMEM)
     planes = message_planes(count)
     strips, send_a, send_b = pl.pallas_call(
         functools.partial(half_kernel, counts=(col_count, flip)),
@@ -605,11 +639,12 @@
     gathered = lax.all_to_all(gram, ("row", "col"), 0, 0, tiled=True)
     updated, last = pl.pallas_call(
         solve_kernel,
-        out_shape=[shapes(*block), shapes(8, LANES)],
+        out_shape=[shapes(*block), shapes(1)],
+        out_specs=[whole, smem],
         compiler_params=VMEM,
         name="solve",
     )(gathered, z, state)
-    return updated, last[0, :1]
+    return updated, last
 
 
 def solution(mesh):

time: 43.3 us -> 38.8 us (0.90)
  local copies, waits for them, and re-layouts: 5.57 us -> 0.1 us
  Pallas kernels: 8.41 us -> 9.57 us
    unnamed x23 -> x3, local copies, waits for them, and re-layouts: 5.06 us -> 0.1 us
    pallas_call x2, Pallas kernels: 2.32 us -> 3.48 us  [the longest x1 2.37 us: body(): pl.pallas_call(pack_kernel, in_specs=[pl.BlockSpec(memory_space=pltpu.HBM...]
    slice x1 -> x0, local copies, waits for them, and re-layouts: 0.51 us -> none  [body(): return (updated, last[0, :1])]
where the time goes in v2:
time: 38.8 us; the launch traced here: 38.6 us
  blocking collectives  11.9 us (31%)
  waiting for transfers between devices  11.8 us (30%)
  Pallas kernels  9.57 us (25%)
  starting transfers between devices  4.6 us (12%)
  between operations  0.66 us (2%)
    all_to_all x1, blocking collectives, body(): gathered = lax.all_to_all(gram, ('row', 'col'), 0, 0, tiled=True)  11.9 us
    ppermute x1, waiting for transfers between devices, body(): got_a = lax.ppermute(send_a, ('parts', 'row'), chain)  6.91 us
    pallas_call x1, Pallas kernels, body(): pl.pallas_call(functools.partial(full_kernel, row_count=row_count, flip=f...  4.43 us
    pallas_call x1, Pallas kernels, body(): pl.pallas_call(pack_kernel, in_specs=[pl.BlockSpec(memory_space=pltpu.HBM...  2.37 us
    ppermute x1, waiting for transfers between devices, body(): from_left = lax.ppermute(to_right, 'col', ring)  2.14 us
    ppermute x1, starting transfers between devices, body(): from_right = lax.ppermute(to_left, 'col', [(b, a) for a, b in ring])  1.98 us
    ppermute x1, waiting for transfers between devices, body(): got_b = lax.ppermute(send_b, ('parts', 'row'), [(b, a) for a, b in chain])  1.86 us
    pallas_call x1, Pallas kernels, body(): pl.pallas_call(functools.partial(half_kernel, counts=(col_count, flip)),...  1.66 us
  transfers between devices with their start and end apart: 4, of which 4 were waited for; matrix products, arithmetic and copies ran while one was open for 0% of the time, Pallas kernels for 0%

profile of v2, /device:TPU:0, one launch (start us, length us, event | category | flops | bytes accessed | tf_op | source)
XLA Modules:
  0.0 38.6 jit_solution(16239220296539135727)
XLA Ops:
  0.6 2.4 %pack_columns.1 = (f32[10,16,128]{2,1,0:T(8,128)S(1)}, f32[10,16,128]{2,1,0:T(8,128)S(1)}, f32[10,10,16,128]{3,2,1,0:T(8,128)S(1)}, f32[10,16,128]{2,1,0:T(8,128...) custom-call(f32[10,16,128]{2,1,0:T(8,128)} %state_in.1, ...), custom_call_target="tpu_custom_call" | custom-call | tf_op jit(solution)/shard_map/pack_columns/pallas_call | solution.py:573
  3.0 0.0 copy-start
  3.0 0.5 %collective-permute-start = (f32[12,16,128]{2,1,0:T(8,128)S(1)}, f32[12,16,128]{2,1,0:T(8,128)S(1)}, u32[]{:S(2)}, u32[]{:S(2)}) collective-permute-start(f32[12,16,128]{2,1,0:T(8,128)S(1)} %get-tuple-element.14), channel_id=1, source_target_pairs={{0,1},{1,2},{2,3},{3,0},{4,5},{5,6},{6,7},{7,4},{8,9},{9,10},{10,1... | collective-permute-start | bytes 294920 | tf_op jit(solution)/shard_map/ppermute | solution.py:586
  3.6 2.0 %collective-permute-start.1 = (f32[12,16,128]{2,1,0:T(8,128)S(1)}, f32[12,16,128]{2,1,0:T(8,128)S(1)}, u32[]{:S(2)}, u32[]{:S(2)}) collective-permute-start(f32[12,16,128]{2,1,0:T(8,128)S(1)} %get-tuple-element.15), channel_id=1, source_target_pairs={{1,0},{2,1},{3,2},{0,3},{5,4},{6,5},{7,6},{4,7},{9,8},{10,9},{11,1... | collective-permute-start | bytes 294920 | tf_op jit(solution)/shard_map/ppermute | solution.py:587
  5.5 0.0 copy-done
  5.5 0.1 copy.10.vel
  5.6 2.1 %collective-permute-done.from_left = f32[12,16,128]{2,1,0:T(8,128)S(1)} collective-permute-done((f32[12,16,128]{2,1,0:T(8,128)S(1)}, f32[12,16,128]{2,1,0:T(8,128)S(1)}, u32[]{:S(2)}, u32[]{:S(2)}) %collective-permute-start) | collective-permute-done | bytes 98336 | tf_op jit(solution)/shard_map/ppermute | solution.py:586
  7.8 0.9 %collective-permute-done.1.from_right = f32[12,16,128]{2,1,0:T(8,128)S(1)} collective-permute-done((f32[12,16,128]{2,1,0:T(8,128)S(1)}, f32[12,16,128]{2,1,0:T(8,128)S(1)}, u32[]{:S(2)}, u32[]{:S(2)}) %collective-permute-start.1) | collective-permute-done | bytes 98336 | tf_op jit(solution)/shard_map/ppermute | solution.py:587
  8.7 1.7 %half_step.1 = (f32[24,16,128]{2,1,0:T(8,128)S(1)}, f32[271,2,128]{2,1,0:T(2,128)S(1)}, f32[271,2,128]{2,1,0:T(2,128)S(1)}) custom-call(f32[12,16,128]{2,1,0:T(8,128)S(1)} %collective-permute-done.from_left, f32[12,16,128]{2,1,0:T(8,128)S(1)} %collective-permute-done.1.from_right, f32[10,16,128]{2,1,0:T(8,128)S(1)} %get-tuple-element.16.state, ...), custom_call_target="tpu_custom_call" | custom-call | tf_op jit(solution)/shard_map/half_step/pallas_call | solution.py:590
  10.3 1.6 %collective-permute-start.2 = (f32[271,2,128]{2,1,0:T(2,128)S(1)}, f32[271,2,128]{2,1,0:T(2,128)S(1)}, u32[]{:S(2)}, u32[]{:S(2)}) collective-permute-start(f32[271,2,128]{2,1,0:T(2,128)S(1)} %get-tuple-element.21), channel_id=1, source_target_pairs={{0,4},{4,8},{8,12},{12,28},{16,0},{20,16},{24,20},{28,24},{1,5},{5... | collective-permute-start | bytes 832520 | tf_op jit(solution)/shard_map/ppermute | solution.py:614
  11.9 0.4 %collective-permute-start.3 = (f32[271,2,128]{2,1,0:T(2,128)S(1)}, f32[271,2,128]{2,1,0:T(2,128)S(1)}, u32[]{:S(2)}, u32[]{:S(2)}) collective-permute-start(f32[271,2,128]{2,1,0:T(2,128)S(1)} %get-tuple-element.22), channel_id=1, source_target_pairs={{4,0},{8,4},{12,8},{28,12},{0,16},{16,20},{20,24},{24,28},{5,1},{9... | collective-permute-start | bytes 832520 | tf_op jit(solution)/shard_map/ppermute | solution.py:615
  12.4 6.9 %collective-permute-done.2.got_a = f32[271,2,128]{2,1,0:T(2,128)S(1)} collective-permute-done((f32[271,2,128]{2,1,0:T(2,128)S(1)}, f32[271,2,128]{2,1,0:T(2,128)S(1)}, u32[]{:S(2)}, u32[]{:S(2)}) %collective-permute-start.2) | collective-permute-done | bytes 277536 | tf_op jit(solution)/shard_map/ppermute | solution.py:614
  19.3 1.9 %collective-permute-done.3.got_b = f32[271,2,128]{2,1,0:T(2,128)S(1)} collective-permute-done((f32[271,2,128]{2,1,0:T(2,128)S(1)}, f32[271,2,128]{2,1,0:T(2,128)S(1)}, u32[]{:S(2)}, u32[]{:S(2)}) %collective-permute-start.3) | collective-permute-done | bytes 277536 | tf_op jit(solution)/shard_map/ppermute | solution.py:615
  21.2 4.4 %krylov.1 = (f32[4,10,16,128]{3,2,1,0:T(8,128)S(1)}, f32[16,128]{1,0:T(8,128)S(1)}) custom-call(f32[271,2,128]{2,1,0:T(2,128)S(1)} %collective-permute-done.2.got_a, f32[271,2,128]{2,1,0:T(2,128)S(1)} %collective-permute-done.3.got_b, f32[24,16,128]{2,1,0:T(8,128)S(1)} %get-tuple-element.23.strips_in, f32[10,16,128]{2,1,0:T(8,128)S(1)} %get-tuple-element.16.state, ...), custom_call_target="tpu_custom_call" | custom-call | tf_op jit(solution)/shard_map/krylov/pallas_call | solution.py:619
  25.6 11.9 %all_to_all.11 = f32[16,1,128]{2,1,0:T(1,128)S(1)} all-to-all(f32[16,1,128]{2,1,0:T(1,128)S(1)} %bitcast.5), channel_id=1, replica_groups=mesh['parts'=2,'row'=4,'col'=4] {'row','col'}, dimensions={0} | all-to-all | bytes 16384 | tf_op jit(solution)/shard_map/all_to_all | solution.py:639
  37.5 1.1 %solve.1 = (f32[10,16,128]{2,1,0:T(8,128)}, f32[1]{0:T(128)}) custom-call(f32[16,128]{1,0:T(8,128)S(1)} %bitcast.4, f32[4,10,16,128]{3,2,1,0:T(8,128)S(1)} %get-tuple-element.25.z_ref, f32[10,16,128]{2,1,0:T(8,128)S(1)} %get-tuple-element.16.state), custom_call_target="tpu_custom_call" | custom-call | tf_op jit(solution)/shard_map/solve/pallas_call | solution.py:640
Async XLA Ops:
  3.0 2.5 %copy-start = (f32[10,2]{0,1:T(2,128)S(1)}, f32[10,2]{0,1:T(2,128)}, u32[]{:S(2)}) copy-start(f32[10,2]{0,1:T(2,128)} %param.10) | copy-start | bytes 244
  3.0 4.8 %collective-permute-start = (f32[12,16,128]{2,1,0:T(8,128)S(1)}, f32[12,16,128]{2,1,0:T(8,128)S(1)}, u32[]{:S(2)}, u32[]{:S(2)}) collective-permute-start(f32[12,16,128]{2,1,0:T(8,128)S(1)} %get-tuple-element.14), channel_id=1, source_target_pairs={{0,1},{1,2},{2,3},{3,0},{4,5},{5,6},{6,7},{7,4},{8,9},{9,10},{10,1... | collective-permute-start | bytes 294920 | tf_op jit(solution)/shard_map/ppermute | solution.py:586
  3.6 5.1 %collective-permute-start.1 = (f32[12,16,128]{2,1,0:T(8,128)S(1)}, f32[12,16,128]{2,1,0:T(8,128)S(1)}, u32[]{:S(2)}, u32[]{:S(2)}) collective-permute-start(f32[12,16,128]{2,1,0:T(8,128)S(1)} %get-tuple-element.15), channel_id=1, source_target_pairs={{1,0},{2,1},{3,2},{0,3},{5,4},{6,5},{7,6},{4,7},{9,8},{10,9},{11,1... | collective-permute-start | bytes 294920 | tf_op jit(solution)/shard_map/ppermute | solution.py:587
  10.3 9.0 %collective-permute-start.2 = (f32[271,2,128]{2,1,0:T(2,128)S(1)}, f32[271,2,128]{2,1,0:T(2,128)S(1)}, u32[]{:S(2)}, u32[]{:S(2)}) collective-permute-start(f32[271,2,128]{2,1,0:T(2,128)S(1)} %get-tuple-element.21), channel_id=1, source_target_pairs={{0,4},{4,8},{8,12},{12,28},{16,0},{20,16},{24,20},{28,24},{1,5},{5... | collective-permute-start | bytes 832520 | tf_op jit(solution)/shard_map/ppermute | solution.py:614
  11.9 9.2 %collective-permute-start.3 = (f32[271,2,128]{2,1,0:T(2,128)S(1)}, f32[271,2,128]{2,1,0:T(2,128)S(1)}, u32[]{:S(2)}, u32[]{:S(2)}) collective-permute-start(f32[271,2,128]{2,1,0:T(2,128)S(1)} %get-tuple-element.22), channel_id=1, source_target_pairs={{4,0},{8,4},{12,8},{28,12},{0,16},{16,20},{20,24},{24,28},{5,1},{9... | collective-permute-start | bytes 832520 | tf_op jit(solution)/shard_map/ppermute | solution.py:615

commit v3 on v2

--- a/solution.py
+++ b/solution.py
@@ -161,9 +161,17 @@
     store(None, (z_s - step_gamma * jac) - v_s)
 
 
+def edge_rows(rows, flip):
+    odd = (lax.axis_index("parts") % 2) if flip else 0
+    down, up = (rows - 2, rows - 3), (0, 2)
+    return tuple(
+        tuple(x + (y - x) * odd for x, y in zip(*ends)) for ends in ((down, up), (up, down))
+    )
+
+
 def pack_kernel(
     state_in, history_in, rates_in, quadratic_in, precond_in,
-    state, history, rates, quadratic, precond, to_right, to_left, sems,
+    state, history, rates, quadratic, precond, to_right, to_left, raw_a, raw_b, sems, *, flip,
 ):
     count, rows, _ = state.shape
     copies = [
@@ -212,6 +220,12 @@
         to_right[pair] = jnp.where(low, roll_lanes(two, -4), one)
         to_left[pair] = jnp.where(low, one, roll_lanes(two, 4))
 
+    for target, (near, _) in zip((raw_a, raw_b), edge_rows(rows, flip)):
+        planes = [m.at[s, t] for m in (rates, precond) for s in range(count) for t in range(count)]
+        planes += [ref.at[s] for ref in (state, quadratic, history) for s in range(count)]
+        for n, ref in enumerate(planes):
+            target[n] = ref[pl.ds(near, 2), :]
+
 
 def half_kernel(
     from_left, from_right, state, history, rates, quadratic, precond, vel,
@@ -258,35 +272,25 @@
     )
     precondition(1)
 
-    odd = (lax.axis_index("parts") % 2) if flip else 0
-    for target, near, far in (
-        (send_a, (rows - 2) * (1 - odd), (rows - 3) * (1 - odd) + 2 * odd),
-        (send_b, (rows - 2) * odd, (rows - 3) * odd + 2 * (1 - odd)),
-    ):
-        base = 0
-        for matrix in (rates, precond):
-            for s in range(count):
-                for t in range(count):
-                    target[base] = matrix[s, t, pl.ds(near, 2), :]
-                    base += 1
-        for ref in (state, quadratic, history):
-            for s in range(count):
-                target[base] = ref[s, pl.ds(near, 2), :]
-                base += 1
-        for g in range(2 * count + 4):
-            target[base] = strips_out[g, pl.ds(near, 2), :]
-            base += 1
-        single = [state.at[s] for s in range(count)]
-        single += [z_ref.at[k, s] for k in range(2) for s in range(count)]
-        single += [strips_out.at[2 * count], zs_ref.at[0], zs_ref.at[1]]
+    single = [state.at[s] for s in range(count)]
+    single += [z_ref.at[k, s] for k in range(2) for s in range(count)]
+    single += [strips_out.at[2 * count], zs_ref.at[0], zs_ref.at[1]]
+    base = 2 * count + 4
+    for target, (near, far) in zip((send_a, send_b), edge_rows(rows, flip)):
+        for g in range(base):
+            target[g] = strips_out[g, pl.ds(near, 2), :]
         for j, ref in enumerate(single):
             target[base + j // 2, pl.ds(j % 2, 1), :] = ref[pl.ds(far, 1), :]
         if len(single) % 2:
             target[base + len(single) // 2, pl.ds(1, 1), :] = jnp.zeros((1, LANES), F32)
 
 
+def raw_planes(count):
+    return 2 * count * count + 3 * count
+
+
 def message_planes(count):
-    return 2 * count * count + 3 * count + (2 * count + 4) + (3 * count + 3 + 1) // 2
+    return (2 * count + 4) + (3 * count + 3 + 1) // 2
 
 
 def pairs_of(width):
@@ -294,7 +298,7 @@
 
 
 def full_kernel(
-    got_a, got_b, strips_in, state, history, rates, quadratic, precond, vel,
+    raw_a, raw_b, got_a, got_b, strips_in, state, history, rates, quadratic, precond, vel,
     z_out, gram_out,
     halo_rates, halo_precond, fields_ref, strips_ref, inject_ref, inject_s, v_ref, vs_ref,
     zx_ref, zs_ref, *, row_count, flip,
@@ -310,12 +314,13 @@
     keep_b = below * (1 - odd_f) + above * odd_f
     near_a, far_a = 6 * (1 - odd), 5 * (1 - odd) + 2 * odd
     near_b, far_b = 6 * odd, 5 * odd + 2 * (1 - odd)
+    raws = ((raw_a, keep_a, near_a), (raw_b, keep_b, near_b))
     sources = ((got_a, keep_a, near_a, far_a), (got_b, keep_b, near_b, far_b))
     blank = jnp.zeros((8, LANES), F32)
 
-    def receive(target, base, at=0):
+    def receive(target, base, at=0, sources=raws):
         target[pl.ds(at, 8), :] = blank
-        for source, keep, near, _ in sources:
+        for source, keep, near, *_ in sources:
             target[pl.ds(at + near, 2), :] = source[base] * keep
 
     base = 0
@@ -328,10 +333,10 @@
             fields_ref[f, s, 0:rows, :] = ref[s]
             receive(fields_ref.at[f, s], base, rows)
             base += 1
-    for g in range(2 * count + 4):
+    base = 2 * count + 4
+    for g in range(base):
         strips_ref[g, 0:rows, :] = strips_in[g]
-        receive(strips_ref.at[g], base, rows)
-        base += 1
+        receive(strips_ref.at[g], g, rows, sources)
     single = [(fields_ref.at[0, s], rows) for s in range(count)]
     for k in range(2):
         for s in range(count):
@@ -570,14 +575,17 @@
         pltpu.with_memory_space_constraint(x, pltpu.HBM)
         for x in (state, history, rates, quadratic, precond)
     ]
-    state, history, rates, quadratic, precond, to_right, to_left = pl.pallas_call(
-        pack_kernel,
+    (
+        state, history, rates, quadratic, precond, to_right, to_left, send_a, send_b
+    ) = pl.pallas_call(
+        functools.partial(pack_kernel, flip=flip),
         in_specs=[pl.BlockSpec(memory_space=pltpu.HBM)] * 5,
         out_shape=[
             shapes(*block), shapes(*block), shapes(*square), shapes(*block), shapes(*square),
             shapes(count + 2, rows, LANES), shapes(count + 2, rows, LANES),
+            shapes(raw_planes(count), 2, LANES), shapes(raw_planes(count), 2, LANES),
         ],
-        out_specs=[whole] * 7,
+        out_specs=[whole] * 9,
         scratch_shapes=[pltpu.SemaphoreType.DMA((5,))],
         compiler_params=VMEM,
         name="pack_columns",
@@ -585,6 +593,20 @@
     ring = [(i, (i + 1) % col_count) for i in range(col_count)]
     from_left = lax.ppermute(to_right, "col", ring)
     from_right = lax.ppermute(to_left, "col", [(b, a) for a, b in ring])
+
+    chain = []
+    for p in range(part_count):
+        for r in range(row_count):
+            if flip and p % 2:
+                target = (p, r - 1) if r else (p - 1, 0)
+            elif flip:
+                target = (p, r + 1) if r < row_count - 1 else (p + 1, r)
+            else:
+                target = (p, (r + 1) % row_count)
+            chain.append((p * row_count + r, target[0] * row_count + target[1]))
+    back = [(b, a) for a, b in chain]
+    raw_a = lax.ppermute(send_a, ("parts", "row"), chain)
+    raw_b = lax.ppermute(send_b, ("parts", "row"), back)
 
     planes = message_planes(count)
     strips, send_a, send_b = pl.pallas_call(
@@ -601,24 +623,14 @@
         name="half_step",
     )(from_left, from_right, state, history, rates, quadratic, precond, velocity)
 
-    chain = []
-    for p in range(part_count):
-        for r in range(row_count):
-            if flip and p % 2:
-                target = (p, r - 1) if r else (p - 1, 0)
-            elif flip:
-                target = (p, r + 1) if r < row_count - 1 else (p + 1, r)
-            else:
-                target = (p, (r + 1) % row_count)
-            chain.append((p * row_count + r, target[0] * row_count + target[1]))
     got_a = lax.ppermute(send_a, ("parts", "row"), chain)
-    got_b = lax.ppermute(send_b, ("parts", "row"), [(b, a) for a, b in chain])
+    got_b = lax.ppermute(send_b, ("parts", "row"), back)
 
     ext = rows + 8
     members = row_count * col_count
     z, gram = pl.pallas_call(
         functools.partial(full_kernel, row_count=row_count, flip=flip),
-        in_specs=[whole] * 8 + [smem],
+        in_specs=[whole] * 10 + [smem],
         out_shape=[shapes(KRYLOV, *block), shapes(members, LANES)],
         scratch_shapes=[
             pltpu.VMEM((count * count, 8, LANES), F32),
@@ -634,7 +646,7 @@
         ],
         compiler_params=VMEM,
         name="krylov",
-    )(got_a, got_b, strips, state, history, rates, quadratic, precond, velocity)
+    )(raw_a, raw_b, got_a, got_b, strips, state, history, rates, quadratic, precond, velocity)
 
     gathered = lax.all_to_all(gram, ("row", "col"), 0, 0, tiled=True)
     updated, last = pl.pallas_call(

time: 38.8 us -> 36 us (0.928)
  waiting for transfers between devices: 11.8 us -> 6.27 us
  starting transfers between devices: 4.6 us -> 6.94 us
  blocking collectives: 11.9 us -> 12.4 us
    ppermute x1, waiting for transfers between devices: 6.91 us -> 1.99 us  [body(): got_a = lax.ppermute(send_a, ('parts', 'row'), chain)]
    ppermute x1 -> x3, starting transfers between devices: 0.45 us -> 3.57 us  [the longest x1 3.1 us: body(): raw_a = lax.ppermute(send_a, ('parts', 'row'), chain)]
    ppermute x1, starting transfers between devices: 0.54 us -> 0.01 us  [body(): from_left = lax.ppermute(to_right, 'col', ring)]
    all_to_all x1, blocking collectives: 11.9 us -> 12.4 us  [body(): gathered = lax.all_to_all(gram, ('row', 'col'), 0, 0, tiled=True)]
    ppermute x1 -> x3, waiting for transfers between devices: 1.86 us -> 1.58 us  [the longest x1 1.58 us: body(): got_b = lax.ppermute(send_b, ('parts', 'row'), back)]
  transfers between devices with their start and end apart: 4 -> 6, of which waited for: 4 -> 4; matrix products, arithmetic and copies ran while one was open for 0% -> 0% of each run, Pallas kernels for 0% -> 4%
where the time goes in v3:
time: 36 us; the launch traced here: 35.8 us
  blocking collectives  12.4 us (34%)
  Pallas kernels  9.49 us (26%)
  starting transfers between devices  6.94 us (19%)
  waiting for transfers between devices  6.27 us (17%)
  between operations  0.65 us (2%)
    all_to_all x1, blocking collectives, body(): gathered = lax.all_to_all(gram, ('row', 'col'), 0, 0, tiled=True)  12.4 us
    pallas_call x1, Pallas kernels, body(): pl.pallas_call(functools.partial(full_kernel, row_count=row_count, flip=f...  4.38 us
    ppermute x1, starting transfers between devices, body(): raw_a = lax.ppermute(send_a, ('parts', 'row'), chain)  3.1 us
    pallas_call x1, Pallas kernels, body(): pl.pallas_call(functools.partial(pack_kernel, flip=flip), in_specs=[pl.Bl...  2.44 us
    ppermute x1, waiting for transfers between devices, body(): from_left = lax.ppermute(to_right, 'col', ring)  2.2 us
    ppermute x1, waiting for transfers between devices, body(): got_a = lax.ppermute(send_a, ('parts', 'row'), chain)  1.99 us
    ppermute x1, starting transfers between devices, body(): from_right = lax.ppermute(to_left, 'col', [(b, a) for a, b in ring])  1.74 us
    ppermute x1, starting transfers between devices, body(): got_a = lax.ppermute(send_a, ('parts', 'row'), chain)  1.63 us
  transfers between devices with their start and end apart: 6, of which 4 were waited for; matrix products, arithmetic and copies ran while one was open for 0% of the time, Pallas kernels for 4%

profile of v3, /device:TPU:0, one launch (start us, length us, event | category | flops | bytes accessed | tf_op | source)
XLA Modules:
  0.0 35.8 jit_solution(13216071031568105096)
XLA Ops:
  0.6 2.4 %pack_columns.1 = (f32[10,16,128]{2,1,0:T(8,128)S(1)}, f32[10,16,128]{2,1,0:T(8,128)S(1)}, f32[10,10,16,128]{3,2,1,0:T(8,128)S(1)}, f32[10,16,128]{2,1,0:T(8,128...) custom-call(f32[10,16,128]{2,1,0:T(8,128)} %state_in.1, ...), custom_call_target="tpu_custom_call" | custom-call | tf_op jit(solution)/shard_map/pack_columns/pallas_call | solution.py:580
  3.1 3.1 %collective-permute-start = (f32[230,2,128]{2,1,0:T(2,128)S(1)}, f32[230,2,128]{2,1,0:T(2,128)S(1)}, u32[]{:S(2)}, u32[]{:S(2)}) collective-permute-start(f32[230,2,128]{2,1,0:T(2,128)S(1)} %get-tuple-element.16), channel_id=1, source_target_pairs={{0,4},{4,8},{8,12},{12,28},{16,0},{20,16},{24,20},{28,24},{1,5},{5... | collective-permute-start | bytes 706568 | tf_op jit(solution)/shard_map/ppermute | solution.py:608
  6.2 0.0 collective-permute-start.1
  6.2 0.0 copy-start
  6.2 0.0 collective-permute-start.2
  6.2 1.7 %collective-permute-start.3 = (f32[12,16,128]{2,1,0:T(8,128)S(1)}, f32[12,16,128]{2,1,0:T(8,128)S(1)}, u32[]{:S(2)}, u32[]{:S(2)}) collective-permute-start(f32[12,16,128]{2,1,0:T(8,128)S(1)} %get-tuple-element.19), channel_id=1, source_target_pairs={{1,0},{2,1},{3,2},{0,3},{5,4},{6,5},{7,6},{4,7},{9,8},{10,9},{11,1... | collective-permute-start | bytes 294920 | tf_op jit(solution)/shard_map/ppermute | solution.py:595
  7.9 0.0 copy-done
  8.0 0.1 copy.10.vel
  8.0 2.2 %collective-permute-done.2.from_left = f32[12,16,128]{2,1,0:T(8,128)S(1)} collective-permute-done((f32[12,16,128]{2,1,0:T(8,128)S(1)}, f32[12,16,128]{2,1,0:T(8,128)S(1)}, u32[]{:S(2)}, u32[]{:S(2)}) %collective-permute-start.2) | collective-permute-done | bytes 98336 | tf_op jit(solution)/shard_map/ppermute | solution.py:594
  10.2 0.5 %collective-permute-done.3.from_right = f32[12,16,128]{2,1,0:T(8,128)S(1)} collective-permute-done((f32[12,16,128]{2,1,0:T(8,128)S(1)}, f32[12,16,128]{2,1,0:T(8,128)S(1)}, u32[]{:S(2)}, u32[]{:S(2)}) %collective-permute-start.3) | collective-permute-done | bytes 98336 | tf_op jit(solution)/shard_map/ppermute | solution.py:595
  10.7 1.6 %half_step.1 = (f32[24,16,128]{2,1,0:T(8,128)S(1)}, f32[41,2,128]{2,1,0:T(2,128)S(1)}, f32[41,2,128]{2,1,0:T(2,128)S(1)}) custom-call(f32[12,16,128]{2,1,0:T(8,128)S(1)} %collective-permute-done.2.from_left, f32[12,16,128]{2,1,0:T(8,128)S(1)} %collective-permute-done.3.from_right, f32[10,16,128]{2,1,0:T(8,128)S(1)} %get-tuple-element.20.state, ...), custom_call_target="tpu_custom_call" | custom-call | tf_op jit(solution)/shard_map/half_step/pallas_call | solution.py:612
  12.3 1.6 %collective-permute-start.4 = (f32[41,2,128]{2,1,0:T(2,128)S(1)}, f32[41,2,128]{2,1,0:T(2,128)S(1)}, u32[]{:S(2)}, u32[]{:S(2)}) collective-permute-start(f32[41,2,128]{2,1,0:T(2,128)S(1)} %get-tuple-element.25), channel_id=1, source_target_pairs={{0,4},{4,8},{8,12},{12,28},{16,0},{20,16},{24,20},{28,24},{1,5},{5... | collective-permute-start | bytes 125960 | tf_op jit(solution)/shard_map/ppermute | solution.py:626
  13.9 0.4 %collective-permute-start.5 = (f32[41,2,128]{2,1,0:T(2,128)S(1)}, f32[41,2,128]{2,1,0:T(2,128)S(1)}, u32[]{:S(2)}, u32[]{:S(2)}) collective-permute-start(f32[41,2,128]{2,1,0:T(2,128)S(1)} %get-tuple-element.26), channel_id=1, source_target_pairs={{4,0},{8,4},{12,8},{28,12},{0,16},{16,20},{20,24},{24,28},{5,1},{9... | collective-permute-start | bytes 125960 | tf_op jit(solution)/shard_map/ppermute | solution.py:627
  14.4 2.0 %collective-permute-done.4.got_a = f32[41,2,128]{2,1,0:T(2,128)S(1)} collective-permute-done((f32[41,2,128]{2,1,0:T(2,128)S(1)}, f32[41,2,128]{2,1,0:T(2,128)S(1)}, u32[]{:S(2)}, u32[]{:S(2)}) %collective-permute-start.4) | collective-permute-done | bytes 42016 | tf_op jit(solution)/shard_map/ppermute | solution.py:626
  16.4 1.6 %collective-permute-done.5.got_b = f32[41,2,128]{2,1,0:T(2,128)S(1)} collective-permute-done((f32[41,2,128]{2,1,0:T(2,128)S(1)}, f32[41,2,128]{2,1,0:T(2,128)S(1)}, u32[]{:S(2)}, u32[]{:S(2)}) %collective-permute-start.5) | collective-permute-done | bytes 42016 | tf_op jit(solution)/shard_map/ppermute | solution.py:627
  17.9 0.0 collective-permute-done.raw_a
  17.9 0.0 collective-permute-done.1.raw_b
  18.0 4.4 %krylov.1 = (f32[4,10,16,128]{3,2,1,0:T(8,128)S(1)}, f32[16,128]{1,0:T(8,128)S(1)}) custom-call(f32[230,2,128]{2,1,0:T(2,128)S(1)} %collective-permute-done.raw_a, f32[230,2,128]{2,1,0:T(2,128)S(1)} %collective-permute-done.1.raw_b, f32[41,2,128]{2,1,0:T(2,128)S(1)} %collective-permute-done.4.got_a, f32[41,2,128]{2,1,0:T(2,128)S(1)} %collective-permute-done.5.got_b, ...), custom_call_target="tpu_custom_call" | custom-call | tf_op jit(solution)/shard_map/krylov/pallas_call | solution.py:631
  22.3 12.4 %all_to_all.11 = f32[16,1,128]{2,1,0:T(1,128)S(1)} all-to-all(f32[16,1,128]{2,1,0:T(1,128)S(1)} %bitcast.5), channel_id=1, replica_groups=mesh['parts'=2,'row'=4,'col'=4] {'row','col'}, dimensions={0} | all-to-all | bytes 16384 | tf_op jit(solution)/shard_map/all_to_all | solution.py:651
  34.7 1.1 %solve.1 = (f32[10,16,128]{2,1,0:T(8,128)}, f32[1]{0:T(128)}) custom-call(f32[16,128]{1,0:T(8,128)S(1)} %bitcast.4, f32[4,10,16,128]{3,2,1,0:T(8,128)S(1)} %get-tuple-element.29.z_ref, f32[10,16,128]{2,1,0:T(8,128)S(1)} %get-tuple-element.20.state), custom_call_target="tpu_custom_call" | custom-call | tf_op jit(solution)/shard_map/solve/pallas_call | solution.py:652
Async XLA Ops:
  3.1 14.9 %collective-permute-start = (f32[230,2,128]{2,1,0:T(2,128)S(1)}, f32[230,2,128]{2,1,0:T(2,128)S(1)}, u32[]{:S(2)}, u32[]{:S(2)}) collective-permute-start(f32[230,2,128]{2,1,0:T(2,128)S(1)} %get-tuple-element.16), channel_id=1, source_target_pairs={{0,4},{4,8},{8,12},{12,28},{16,0},{20,16},{24,20},{28,24},{1,5},{5... | collective-permute-start | bytes 706568 | tf_op jit(solution)/shard_map/ppermute | solution.py:608
  6.2 11.8 %collective-permute-start.1 = (f32[230,2,128]{2,1,0:T(2,128)S(1)}, f32[230,2,128]{2,1,0:T(2,128)S(1)}, u32[]{:S(2)}, u32[]{:S(2)}) collective-permute-start(f32[230,2,128]{2,1,0:T(2,128)S(1)} %get-tuple-element.17), channel_id=1, source_target_pairs={{4,0},{8,4},{12,8},{28,12},{0,16},{16,20},{20,24},{24,28},{5,1},{9... | collective-permute-start | bytes 706568 | tf_op jit(solution)/shard_map/ppermute | solution.py:609
  6.2 1.8 %copy-start = (f32[10,2]{0,1:T(2,128)S(1)}, f32[10,2]{0,1:T(2,128)}, u32[]{:S(2)}) copy-start(f32[10,2]{0,1:T(2,128)} %param.10) | copy-start | bytes 244
  6.2 4.0 %collective-permute-start.2 = (f32[12,16,128]{2,1,0:T(8,128)S(1)}, f32[12,16,128]{2,1,0:T(8,128)S(1)}, u32[]{:S(2)}, u32[]{:S(2)}) collective-permute-start(f32[12,16,128]{2,1,0:T(8,128)S(1)} %get-tuple-element.18), channel_id=1, source_target_pairs={{0,1},{1,2},{2,3},{3,0},{4,5},{5,6},{6,7},{7,4},{8,9},{9,10},{10,1... | collective-permute-start | bytes 294920 | tf_op jit(solution)/shard_map/ppermute | solution.py:594
  6.2 4.5 %collective-permute-start.3 = (f32[12,16,128]{2,1,0:T(8,128)S(1)}, f32[12,16,128]{2,1,0:T(8,128)S(1)}, u32[]{:S(2)}, u32[]{:S(2)}) collective-permute-start(f32[12,16,128]{2,1,0:T(8,128)S(1)} %get-tuple-element.19), channel_id=1, source_target_pairs={{1,0},{2,1},{3,2},{0,3},{5,4},{6,5},{7,6},{4,7},{9,8},{10,9},{11,1... | collective-permute-start | bytes 294920 | tf_op jit(solution)/shard_map/ppermute | solution.py:595
  12.3 4.1 %collective-permute-start.4 = (f32[41,2,128]{2,1,0:T(2,128)S(1)}, f32[41,2,128]{2,1,0:T(2,128)S(1)}, u32[]{:S(2)}, u32[]{:S(2)}) collective-permute-start(f32[41,2,128]{2,1,0:T(2,128)S(1)} %get-tuple-element.25), channel_id=1, source_target_pairs={{0,4},{4,8},{8,12},{12,28},{16,0},{20,16},{24,20},{28,24},{1,5},{5... | collective-permute-start | bytes 125960 | tf_op jit(solution)/shard_map/ppermute | solution.py:626
  13.9 4.0 %collective-permute-start.5 = (f32[41,2,128]{2,1,0:T(2,128)S(1)}, f32[41,2,128]{2,1,0:T(2,128)S(1)}, u32[]{:S(2)}, u32[]{:S(2)}) collective-permute-start(f32[41,2,128]{2,1,0:T(2,128)S(1)} %get-tuple-element.26), channel_id=1, source_target_pairs={{4,0},{8,4},{12,8},{28,12},{0,16},{16,20},{20,24},{24,28},{5,1},{9... | collective-permute-start | bytes 125960 | tf_op jit(solution)/shard_map/ppermute | solution.py:627

commit v4 on v3

--- a/solution.py
+++ b/solution.py
@@ -91,14 +91,16 @@
     return -0.5 * (vx * along_x + vy * (right - left))
 
 
-def strip_speed(vel, count, rows):
+def speeds(vel, count, rows):
     slot = slot_of(rows)
-    vx = jnp.zeros((rows, LANES), F32)
-    vy = jnp.zeros((rows, LANES), F32)
+    mains = [
+        tuple(jnp.broadcast_to(vel[s : s + 1, d : d + 1], (rows, LANES)) for d in range(2))
+        for s in range(count)
+    ]
+    strip = [jnp.zeros((rows, LANES), F32)] * 2
     for s in range(count):
-        vx = jnp.where(slot == s, vel[s, 0], vx)
-        vy = jnp.where(slot == s, vel[s, 1], vy)
-    return vx, vy
+        strip = [jnp.where(slot == s, x, y) for x, y in zip(mains[s], strip)]
+    return mains, strip
 
 
 def spread(strip, t):
@@ -136,7 +138,7 @@
     ), strips(2 * count + 3)
     for s in range(count):
         left, right = move_main(state[s], state_s, s)
-        forcing = drift(state[s], left, right, vel[s, 0], vel[s, 1])
+        forcing = drift(state[s], left, right, *vel[s])
         forcing = forcing + row_product(rates, halo_rates, state, s)
         forcing = forcing - quad[s] * state[s] * state[s]
         store(s, -(state[s] - hist[s] - step_gamma * forcing))
@@ -151,7 +153,7 @@
     count = len(z)
     for s in range(count):
         left, right = move_main(z[s], z_s[...], s)
-        jac = drift(z[s], left, right, vel[s, 0], vel[s, 1])
+        jac = drift(z[s], left, right, *vel[s])
         jac = jac + row_product(rates, halo_rates, z, s) - damp(s) * z[s]
         store(s, (z[s] - step_gamma * jac) - v[s])
     z_s = z_s[...]
@@ -243,7 +245,7 @@
         strips_out[2 * pair] = jnp.where(low, right, left)
         strips_out[2 * pair + 1] = jnp.where(low, roll_lanes(right, -4), roll_lanes(left, 4))
 
-    speed = strip_speed(vel, count, rows)
+    vel, speed = speeds(vel, count, rows)
     strips = lambda g: strips_out[g]
     fields = [[ref[s] for s in range(count)] for ref in (state, quadratic, history)]
 
@@ -253,6 +255,7 @@
                 vs_ref[k] = value
             else:
                 v_ref[k, s] = value
+
         return store
 
     def precondition(k):
@@ -350,7 +353,7 @@
         for source, keep, _, far in sources:
             target[pl.ds(at + far, 1), :] = source[base + j // 2, pl.ds(j % 2, 1), :] * keep
 
-    speed = strip_speed(vel, count, ext)
+    vel, speed = speeds(vel, count, ext)
     strips = lambda g: strips_ref[g]
 
     def put(k):
@@ -359,6 +362,7 @@
                 vs_ref[k] = value
             else:
                 v_ref[k, s] = value
+
         return store
 
     fields = [[fields_ref[f, s] for s in range(count)] for f in range(3)]
@@ -461,7 +465,6 @@
     back = [jnp.where(n > 0.0, 1.0 / jnp.where(n > 0.0, n, 1.0), 0.0) for n in norm]
     inv = {}
     for j in range(KRYLOV):
-        column = {j: None}
         inv[j, j] = back[j]
         for i in reversed(range(j)):
             total = unit[i, j] * back[j]
@@ -611,7 +614,7 @@
     planes = message_planes(count)
     strips, send_a, send_b = pl.pallas_call(
         functools.partial(half_kernel, counts=(col_count, flip)),
-        in_specs=[whole] * 7 + [smem],
+        in_specs=[whole] * 8,
         out_shape=[shapes(2 * count + 4, rows, LANES)] + [shapes(planes, 2, LANES)] * 2,
         scratch_shapes=[
             pltpu.VMEM((2,) + block, F32),
@@ -630,7 +633,7 @@
     members = row_count * col_count
     z, gram = pl.pallas_call(
         functools.partial(full_kernel, row_count=row_count, flip=flip),
-        in_specs=[whole] * 10 + [smem],
+        in_specs=[whole] * 11,
         out_shape=[shapes(KRYLOV, *block), shapes(members, LANES)],
         scratch_shapes=[
             pltpu.VMEM((count * count, 8, LANES), F32),

time: 36 us -> 34.7 us (0.964)
  Pallas kernels: 9.49 us -> 8.21 us
    pallas_call x1, Pallas kernels: 4.38 us -> 3.72 us  [body(): pl.pallas_call(functools.partial(full_kernel, row_count=row_count, flip=f...]
    pallas_call x1, Pallas kernels: 1.55 us -> 0.93 us  [body(): pl.pallas_call(functools.partial(half_kernel, counts=(col_count, flip)),...]
  transfers between devices with their start and end apart: 6 -> 6, of which waited for: 4 -> 4; matrix products, arithmetic and copies ran while one was open for 0% -> 0% of each run, Pallas kernels for 4% -> 3%
where the time goes in v4:
time: 34.7 us; the launch traced here: 34.5 us
  blocking collectives  12.4 us (36%)
  Pallas kernels  8.21 us (24%)
  starting transfers between devices  6.94 us (20%)
  waiting for transfers between devices  6.27 us (18%)
  between operations  0.65 us (2%)
    all_to_all x1, blocking collectives, body(): gathered = lax.all_to_all(gram, ('row', 'col'), 0, 0, tiled=True)  12.4 us
    pallas_call x1, Pallas kernels, body(): pl.pallas_call(functools.partial(full_kernel, row_count=row_count, flip=f...  3.72 us
    ppermute x1, starting transfers between devices, body(): raw_a = lax.ppermute(send_a, ('parts', 'row'), chain)  3.1 us
    pallas_call x1, Pallas kernels, body(): pl.pallas_call(functools.partial(pack_kernel, flip=flip), in_specs=[pl.Bl...  2.44 us
    ppermute x1, waiting for transfers between devices, body(): from_left = lax.ppermute(to_right, 'col', ring)  2.2 us
    ppermute x1, waiting for transfers between devices, body(): got_a = lax.ppermute(send_a, ('parts', 'row'), chain)  1.99 us
    ppermute x1, starting transfers between devices, body(): from_right = lax.ppermute(to_left, 'col', [(b, a) for a, b in ring])  1.74 us
    ppermute x1, starting transfers between devices, body(): got_a = lax.ppermute(send_a, ('parts', 'row'), chain)  1.63 us
  transfers between devices with their start and end apart: 6, of which 4 were waited for; matrix products, arithmetic and copies ran while one was open for 0% of the time, Pallas kernels for 3%

profile of v4, /device:TPU:0, one launch (start us, length us, event | category | flops | bytes accessed | tf_op | source)
XLA Modules:
  0.0 34.5 jit_solution(13955794325229492170)
XLA Ops:
  0.6 2.4 %pack_columns.1 = (f32[10,16,128]{2,1,0:T(8,128)S(1)}, f32[10,16,128]{2,1,0:T(8,128)S(1)}, f32[10,10,16,128]{3,2,1,0:T(8,128)S(1)}, f32[10,16,128]{2,1,0:T(8,128...) custom-call(f32[10,16,128]{2,1,0:T(8,128)} %state_in.1, ...), custom_call_target="tpu_custom_call" | custom-call | tf_op jit(solution)/shard_map/pack_columns/pallas_call | solution.py:583
  3.1 3.1 %collective-permute-start = (f32[230,2,128]{2,1,0:T(2,128)S(1)}, f32[230,2,128]{2,1,0:T(2,128)S(1)}, u32[]{:S(2)}, u32[]{:S(2)}) collective-permute-start(f32[230,2,128]{2,1,0:T(2,128)S(1)} %get-tuple-element.16), channel_id=1, source_target_pairs={{0,4},{4,8},{8,12},{12,28},{16,0},{20,16},{24,20},{28,24},{1,5},{5... | collective-permute-start | bytes 706568 | tf_op jit(solution)/shard_map/ppermute | solution.py:611
  6.2 0.0 collective-permute-start.1
  6.2 0.0 copy-start
  6.2 0.0 collective-permute-start.2
  6.2 1.7 %collective-permute-start.3 = (f32[12,16,128]{2,1,0:T(8,128)S(1)}, f32[12,16,128]{2,1,0:T(8,128)S(1)}, u32[]{:S(2)}, u32[]{:S(2)}) collective-permute-start(f32[12,16,128]{2,1,0:T(8,128)S(1)} %get-tuple-element.19), channel_id=1, source_target_pairs={{1,0},{2,1},{3,2},{0,3},{5,4},{6,5},{7,6},{4,7},{9,8},{10,9},{11,1... | collective-permute-start | bytes 294920 | tf_op jit(solution)/shard_map/ppermute | solution.py:598
  7.9 0.0 copy-done
  8.0 0.1 copy.10.vel
  8.0 2.2 %collective-permute-done.2.from_left = f32[12,16,128]{2,1,0:T(8,128)S(1)} collective-permute-done((f32[12,16,128]{2,1,0:T(8,128)S(1)}, f32[12,16,128]{2,1,0:T(8,128)S(1)}, u32[]{:S(2)}, u32[]{:S(2)}) %collective-permute-start.2) | collective-permute-done | bytes 98336 | tf_op jit(solution)/shard_map/ppermute | solution.py:597
  10.2 0.5 %collective-permute-done.3.from_right = f32[12,16,128]{2,1,0:T(8,128)S(1)} collective-permute-done((f32[12,16,128]{2,1,0:T(8,128)S(1)}, f32[12,16,128]{2,1,0:T(8,128)S(1)}, u32[]{:S(2)}, u32[]{:S(2)}) %collective-permute-start.3) | collective-permute-done | bytes 98336 | tf_op jit(solution)/shard_map/ppermute | solution.py:598
  10.7 0.9 %half_step.1 = (f32[24,16,128]{2,1,0:T(8,128)S(1)}, f32[41,2,128]{2,1,0:T(2,128)S(1)}, f32[41,2,128]{2,1,0:T(2,128)S(1)}) custom-call(f32[12,16,128]{2,1,0:T(8,128)S(1)} %collective-permute-done.2.from_left, f32[12,16,128]{2,1,0:T(8,128)S(1)} %collective-permute-done.3.from_right, f32[10,16,128]{2,1,0:T(8,128)S(1)} %get-tuple-element.20.state, ...), custom_call_target="tpu_custom_call" | custom-call | tf_op jit(solution)/shard_map/half_step/pallas_call | solution.py:615
  11.7 1.6 %collective-permute-start.4 = (f32[41,2,128]{2,1,0:T(2,128)S(1)}, f32[41,2,128]{2,1,0:T(2,128)S(1)}, u32[]{:S(2)}, u32[]{:S(2)}) collective-permute-start(f32[41,2,128]{2,1,0:T(2,128)S(1)} %get-tuple-element.25), channel_id=1, source_target_pairs={{0,4},{4,8},{8,12},{12,28},{16,0},{20,16},{24,20},{28,24},{1,5},{5... | collective-permute-start | bytes 125960 | tf_op jit(solution)/shard_map/ppermute | solution.py:629
  13.3 0.4 %collective-permute-start.5 = (f32[41,2,128]{2,1,0:T(2,128)S(1)}, f32[41,2,128]{2,1,0:T(2,128)S(1)}, u32[]{:S(2)}, u32[]{:S(2)}) collective-permute-start(f32[41,2,128]{2,1,0:T(2,128)S(1)} %get-tuple-element.26), channel_id=1, source_target_pairs={{4,0},{8,4},{12,8},{28,12},{0,16},{16,20},{20,24},{24,28},{5,1},{9... | collective-permute-start | bytes 125960 | tf_op jit(solution)/shard_map/ppermute | solution.py:630
  13.8 2.0 %collective-permute-done.4.got_a = f32[41,2,128]{2,1,0:T(2,128)S(1)} collective-permute-done((f32[41,2,128]{2,1,0:T(2,128)S(1)}, f32[41,2,128]{2,1,0:T(2,128)S(1)}, u32[]{:S(2)}, u32[]{:S(2)}) %collective-permute-start.4) | collective-permute-done | bytes 42016 | tf_op jit(solution)/shard_map/ppermute | solution.py:629
  15.7 1.6 %collective-permute-done.5.got_b = f32[41,2,128]{2,1,0:T(2,128)S(1)} collective-permute-done((f32[41,2,128]{2,1,0:T(2,128)S(1)}, f32[41,2,128]{2,1,0:T(2,128)S(1)}, u32[]{:S(2)}, u32[]{:S(2)}) %collective-permute-start.5) | collective-permute-done | bytes 42016 | tf_op jit(solution)/shard_map/ppermute | solution.py:630
  17.3 0.0 collective-permute-done.raw_a
  17.3 0.0 collective-permute-done.1.raw_b
  17.3 3.7 %krylov.1 = (f32[4,10,16,128]{3,2,1,0:T(8,128)S(1)}, f32[16,128]{1,0:T(8,128)S(1)}) custom-call(f32[230,2,128]{2,1,0:T(2,128)S(1)} %collective-permute-done.raw_a, f32[230,2,128]{2,1,0:T(2,128)S(1)} %collective-permute-done.1.raw_b, f32[41,2,128]{2,1,0:T(2,128)S(1)} %collective-permute-done.4.got_a, f32[41,2,128]{2,1,0:T(2,128)S(1)} %collective-permute-done.5.got_b, ...), custom_call_target="tpu_custom_call" | custom-call | tf_op jit(solution)/shard_map/krylov/pallas_call | solution.py:634
  21.0 12.4 %all_to_all.11 = f32[16,1,128]{2,1,0:T(1,128)S(1)} all-to-all(f32[16,1,128]{2,1,0:T(1,128)S(1)} %bitcast.5), channel_id=1, replica_groups=mesh['parts'=2,'row'=4,'col'=4] {'row','col'}, dimensions={0} | all-to-all | bytes 16384 | tf_op jit(solution)/shard_map/all_to_all | solution.py:654
  33.4 1.1 %solve.1 = (f32[10,16,128]{2,1,0:T(8,128)}, f32[1]{0:T(128)}) custom-call(f32[16,128]{1,0:T(8,128)S(1)} %bitcast.4, f32[4,10,16,128]{3,2,1,0:T(8,128)S(1)} %get-tuple-element.29.z_ref, f32[10,16,128]{2,1,0:T(8,128)S(1)} %get-tuple-element.20.state), custom_call_target="tpu_custom_call" | custom-call | tf_op jit(solution)/shard_map/solve/pallas_call | solution.py:655
Async XLA Ops:
  3.1 14.2 %collective-permute-start = (f32[230,2,128]{2,1,0:T(2,128)S(1)}, f32[230,2,128]{2,1,0:T(2,128)S(1)}, u32[]{:S(2)}, u32[]{:S(2)}) collective-permute-start(f32[230,2,128]{2,1,0:T(2,128)S(1)} %get-tuple-element.16), channel_id=1, source_target_pairs={{0,4},{4,8},{8,12},{12,28},{16,0},{20,16},{24,20},{28,24},{1,5},{5... | collective-permute-start | bytes 706568 | tf_op jit(solution)/shard_map/ppermute | solution.py:611
  6.2 11.1 %collective-permute-start.1 = (f32[230,2,128]{2,1,0:T(2,128)S(1)}, f32[230,2,128]{2,1,0:T(2,128)S(1)}, u32[]{:S(2)}, u32[]{:S(2)}) collective-permute-start(f32[230,2,128]{2,1,0:T(2,128)S(1)} %get-tuple-element.17), channel_id=1, source_target_pairs={{4,0},{8,4},{12,8},{28,12},{0,16},{16,20},{20,24},{24,28},{5,1},{9... | collective-permute-start | bytes 706568 | tf_op jit(solution)/shard_map/ppermute | solution.py:612
  6.2 1.8 %copy-start = (f32[10,2]{0,1:T(2,128)S(1)}, f32[10,2]{0,1:T(2,128)}, u32[]{:S(2)}) copy-start(f32[10,2]{0,1:T(2,128)} %param.10) | copy-start | bytes 244
  6.2 4.0 %collective-permute-start.2 = (f32[12,16,128]{2,1,0:T(8,128)S(1)}, f32[12,16,128]{2,1,0:T(8,128)S(1)}, u32[]{:S(2)}, u32[]{:S(2)}) collective-permute-start(f32[12,16,128]{2,1,0:T(8,128)S(1)} %get-tuple-element.18), channel_id=1, source_target_pairs={{0,1},{1,2},{2,3},{3,0},{4,5},{5,6},{6,7},{7,4},{8,9},{9,10},{10,1... | collective-permute-start | bytes 294920 | tf_op jit(solution)/shard_map/ppermute | solution.py:597
  6.2 4.5 %collective-permute-start.3 = (f32[12,16,128]{2,1,0:T(8,128)S(1)}, f32[12,16,128]{2,1,0:T(8,128)S(1)}, u32[]{:S(2)}, u32[]{:S(2)}) collective-permute-start(f32[12,16,128]{2,1,0:T(8,128)S(1)} %get-tuple-element.19), channel_id=1, source_target_pairs={{1,0},{2,1},{3,2},{0,3},{5,4},{6,5},{7,6},{4,7},{9,8},{10,9},{11,1... | collective-permute-start | bytes 294920 | tf_op jit(solution)/shard_map/ppermute | solution.py:598
  11.7 4.1 %collective-permute-start.4 = (f32[41,2,128]{2,1,0:T(2,128)S(1)}, f32[41,2,128]{2,1,0:T(2,128)S(1)}, u32[]{:S(2)}, u32[]{:S(2)}) collective-permute-start(f32[41,2,128]{2,1,0:T(2,128)S(1)} %get-tuple-element.25), channel_id=1, source_target_pairs={{0,4},{4,8},{8,12},{12,28},{16,0},{20,16},{24,20},{28,24},{1,5},{5... | collective-permute-start | bytes 125960 | tf_op jit(solution)/shard_map/ppermute | solution.py:629
  13.3 4.0 %collective-permute-start.5 = (f32[41,2,128]{2,1,0:T(2,128)S(1)}, f32[41,2,128]{2,1,0:T(2,128)S(1)}, u32[]{:S(2)}, u32[]{:S(2)}) collective-permute-start(f32[41,2,128]{2,1,0:T(2,128)S(1)} %get-tuple-element.26), channel_id=1, source_target_pairs={{4,0},{8,4},{12,8},{28,12},{0,16},{16,20},{20,24},{24,28},{5,1},{9... | collective-permute-start | bytes 125960 | tf_op jit(solution)/shard_map/ppermute | solution.py:630

commit v5 on v4

v5 whole, which is shorter than its diff:
```python
import functools

import jax
import jax.numpy as jnp
from jax import lax
from jax.experimental import pallas as pl
from jax.experimental.pallas import tpu as pltpu
from jax.sharding import PartitionSpec as P

KRYLOV = 4
step_gamma = 0.4
tiny_eps = 1e-12

F32 = jnp.float32
LANES = 128
VMEM = pltpu.CompilerParams(vmem_limit_bytes=48 * 1024 * 1024)


def lane_of(rows):
    return lax.broadcasted_iota(jnp.int32, (rows, LANES), 1)


def row_of(rows):
    return lax.broadcasted_iota(jnp.int32, (rows, LANES), 0)


def roll_lanes(x, shift):
    shift %= LANES
    return pltpu.roll(x, shift, 1) if shift else x


def roll_rows(x, shift):
    return pltpu.roll(x, shift % x.shape[0], 0)


def slot_of(rows):
    return ((131 - lane_of(rows)) // 8) % 16


def two_sum(a, b):
    s = a + b
    t = s - a
    return s, (a - (s - t)) + (b - t)


def quick_sum(a, b):
    s = a + b
    return s, b - (s - a)


def split(a):
    c = a * 4097.0
    high = c - (c - a)
    return high, a - high


def two_prod(a, b):
    p = a * b
    ah, al = split(a)
    bh, bl = split(b)
    return p, ((ah * bh - p) + ah * bl + al * bh) + al * bl


def tile_rows(n):
    return slice(8 * n, 8 * n + 8)


def vertical(field, n):
    tiles = field.shape[0] // 8
    this = field[tile_rows(n), :]
    following = field[tile_rows((n + 1) % tiles), :]
    leading = field[tile_rows((n - 1) % tiles), :]
    row = row_of(8)
    under = roll_rows(jnp.where(row == 0, following, this), -1)
    over = roll_rows(jnp.where(row == 7, leading, this), 1)
    return under - over


def speeds(vel, count):
    slot = slot_of(8)
    mains = [
        tuple(
            jnp.broadcast_to(0.5 * step_gamma * vel[s : s + 1, d : d + 1], (8, LANES))
            for d in range(2)
        )
        for s in range(count)
    ]
    strip = [jnp.zeros((8, LANES), F32)] * 2
    for s in range(count):
        strip = [jnp.where(slot == s, x, y) for x, y in zip(mains[s], strip)]
    return mains, strip


def diagonals(count):
    return range(-((count - 1) // 2), count // 2 + 1)


def sum_of(terms):
    return functools.reduce(jnp.add, terms)


def products(tile, fields):
    span = range(len(fields))
    return [sum_of([tile(s, t) * fields[t] for t in span]) for s in span]


def strip_product(strips, base, n, strip, count):
    slot = slot_of(8)
    past_end = jnp.where(slot < count, strip, roll_lanes(strip, -8 * count))
    past_start = jnp.where(slot < count, strip, roll_lanes(strip, -8 * (16 - count)))
    return sum_of(
        [
            strips[base + g, tile_rows(n), :] * roll_lanes(past_end if d >= 0 else past_start, 8 * d)
            for g, d in enumerate(diagonals(count))
        ]
    )


def drift(ring, ring_s, n, speed, count, second=None, with_strip=True):
    vel, vel_s = speed
    lane, slot = lane_of(8), slot_of(8)
    strip = ring_s[tile_rows(n), :]
    edge = jnp.zeros((8, LANES), F32)
    mains, moved = [], []
    for s in range(count):
        main = ring[s, tile_rows(n), :]
        outer = roll_lanes(strip, 8 * s)
        left = roll_lanes(jnp.where(lane == LANES - 1, outer, main), 1)
        right = roll_lanes(jnp.where(lane == 0, outer, main), -1)
        along_x = vertical(ring.at[s], n)
        moved.append(vel[s][0] * along_x + vel[s][1] * (right - left))
        if with_strip:
            edge = jnp.where(slot == s, roll_lanes(main, -8 * s), edge)
        mains.append(main)
    if not with_strip:
        return mains, strip, moved, None
    left = roll_lanes(jnp.where(lane % 8 == 7, edge, strip), 1)
    right = roll_lanes(jnp.where(lane % 8 == 0, edge, strip), -1)
    if second is not None:
        left = jnp.where(lane % 8 == 4, roll_lanes(second, -3), left)
        right = jnp.where(lane % 8 == 3, roll_lanes(second, 3), right)
    along_x = vertical(ring_s, n)
    return mains, strip, moved, vel_s[0] * along_x + vel_s[1] * (right - left)


def first_vector(n, state_ring, state_ring_s, quad, hist, rates, strips, speed, count, put, damp):
    base = 2 * count
    second = strips[base + 3, tile_rows(n), :]
    state, strip, moved, moved_s = drift(state_ring, state_ring_s, n, speed, count, second)
    linear = products(rates, state)
    for s in range(count):
        loss = step_gamma * quad(s) * state[s]
        damp(s, 1.0 + 2.0 * loss)
        put(s, ((hist(s) - state[s]) - moved[s]) + (step_gamma * linear[s] - loss * state[s]))
    linear = strip_product(strips, 0, n, strip, count)
    loss = step_gamma * strips[base + 1, tile_rows(n), :] * strip
    damp(None, 1.0 + 2.0 * loss)
    past = strips[base + 2, tile_rows(n), :]
    put(None, ((past - strip) - moved_s) + (step_gamma * linear - loss * strip))


def next_vector(n, ring, ring_s, old, rates, strips, speed, count, put, damp, with_strip=True):
    z, strip, moved, moved_s = drift(ring, ring_s, n, speed, count, None, with_strip)
    linear = products(rates, z)
    for s in range(count):
        put(s, ((damp(s) * z[s] - old(s)) + moved[s]) - step_gamma * linear[s])
    if with_strip:
        linear = strip_product(strips, 0, n, strip, count)
        put(None, ((damp(None) * strip - old(None)) + moved_s) - step_gamma * linear)


def odd_part(flip):
    return lax.axis_index("parts") % 2 if flip else jnp.int32(0)


def edge_rows(rows, flip):
    odd = odd_part(flip)
    down, up = (rows - 2, rows - 3), (0, 2)
    return tuple(
        tuple(x + (y - x) * odd for x, y in zip(*ends)) for ends in ((down, up), (up, down))
    )


def pack_kernel(
    state_in, history_in, rates_in, quadratic_in, precond_in,
    state, history, rates, quadratic, precond, edge_a, edge_b, raw_a, raw_b, sems, *, flip,
):
    count, rows, _ = state.shape
    copies = [
        pltpu.make_async_copy(source, target, sems.at[n])
        for n, (source, target) in enumerate(
            (
                (rates_in, rates),
                (precond_in, precond),
                (state_in, state),
                (quadratic_in, quadratic),
                (history_in, history),
            )
        )
    ]
    for copy in copies:
        copy.start()
    odd = odd_part(flip) == 1
    slot = slot_of(rows)
    low = lane_of(rows) % 8 < 4

    def group(index):
        packed = jnp.zeros((rows, LANES), F32)
        for s in range(count):
            if index < 2 * count:
                other = (s + diagonals(count)[index % count]) % count
                plane = (rates if index < count else precond)[s, other]
            else:
                plane = (state, quadratic, history, state)[index - 2 * count][s]
            if index == 2 * count + 3:
                moved = jnp.where(
                    low, roll_lanes(plane, -4 - 8 * s), roll_lanes(plane, 4 - 8 * s)
                )
            else:
                moved = roll_lanes(plane, -8 * s)
            packed = jnp.where(slot == s, moved, packed)
        return packed

    done = set()
    for pair in range(count + 2):
        ready = 1 if 2 * pair + 1 < count else 2 if 2 * pair + 1 < 2 * count else 5
        for n in range(ready):
            if n not in done:
                copies[n].wait()
                done.add(n)
        one, two = group(2 * pair), group(2 * pair + 1)
        right = jnp.where(low, roll_lanes(two, -4), one)
        left = jnp.where(low, one, roll_lanes(two, 4))
        edge_a[pair] = right
        edge_b[pair] = left

    for target, (near, _) in zip((raw_a, raw_b), edge_rows(rows, flip)):
        planes = [m.at[s, t] for m in (rates, precond) for s in range(count) for t in range(count)]
        planes += [ref.at[s] for ref in (state, quadratic, history) for s in range(count)]
        for n, ref in enumerate(planes):
            target[n] = ref[pl.ds(near, 2), :]


def half_kernel(
    edge_a, edge_b, state, history, rates, quadratic, precond, vel,
    strips, send_a, send_b,
    state_ring, state_ring_s, damp_ref, damp_s, v_ref, v_s, ring, ring_s, *, counts,
):
    count, rows, _ = state.shape
    cols, flip = counts
    tiles = rows // 8
    low = lane_of(rows) % 8 < 4
    odd = odd_part(flip) == 1
    position = lax.axis_index("col")
    has_left = (position > 0).astype(F32)
    has_right = (position < cols - 1).astype(F32)
    for pair in range(count + 2):
        a, b = edge_a[pair], edge_b[pair]
        left = a * has_left
        right = b * has_right
        strips[2 * pair] = jnp.where(low, right, left)
        strips[2 * pair + 1] = jnp.where(low, roll_lanes(right, -4), roll_lanes(left, 4))

    speed = speeds(vel, count)
    for n in range(tiles):
        for s in range(count):
            state_ring.at[s][tile_rows(n), :] = state[s, tile_rows(n), :]
        state_ring_s[tile_rows(n), :] = strips[2 * count, tile_rows(n), :]

    def putter(main, strip, n):
        def put(s, value):
            if s is None:
                strip[tile_rows(n), :] = value
            else:
                main[s, tile_rows(n), :] = value

        return put

    def getter(main, strip, n):
        return lambda s: strip[tile_rows(n), :] if s is None else main[s, tile_rows(n), :]

    def condition(k):
        for n in range(tiles):
            v = [v_ref[s, tile_rows(n), :] for s in range(count)]
            z = products(lambda s, t: precond[s, t, tile_rows(n), :], v)
            for s in range(count):
                ring.at[k, s][tile_rows(n), :] = z[s]
            z_s = strip_product(strips, count, n, v_s[tile_rows(n), :], count)
            ring_s.at[k][tile_rows(n), :] = z_s

    for n in range(tiles):
        first_vector(
            n, state_ring, state_ring_s,
            lambda s: quadratic[s, tile_rows(n), :], lambda s: history[s, tile_rows(n), :],
            lambda s, t: rates[s, t, tile_rows(n), :], strips, speed, count,
            putter(v_ref, v_s, n), putter(damp_ref, damp_s, n),
        )
    condition(0)
    for n in range(tiles):
        next_vector(
            n, ring.at[0], ring_s.at[0], getter(v_ref, v_s, n),
            lambda s, t: rates[s, t, tile_rows(n), :], strips, speed, count,
            putter(v_ref, v_s, n), getter(damp_ref, damp_s, n),
        )
    condition(1)

    single = [state.at[s] for s in range(count)]
    single += [ring.at[k, s] for k in range(2) for s in range(count)]
    single += [strips.at[2 * count]] + [ring_s.at[k] for k in range(2)]
    base = 2 * count + 4
    for target, (near, far) in zip((send_a, send_b), edge_rows(rows, flip)):
        for g in range(base):
            target[g] = strips[g, pl.ds(near, 2), :]
        for j, ref in enumerate(single):
            target[base + j // 2, pl.ds(j % 2, 1), :] = ref[pl.ds(far, 1), :]
        if len(single) % 2:
            target[base + len(single) // 2, pl.ds(1, 1), :] = jnp.zeros((1, LANES), F32)


def raw_planes(count):
    return 2 * count * count + 3 * count


def message_planes(count):
    return (2 * count + 4) + (3 * count + 3 + 1) // 2


def pairs_of(width):
    return [(i, j) for i in range(width) for j in range(i, width)]


def full_kernel(
    raw_a, raw_b, got_a, got_b, strips_in, state, history, rates, quadratic, precond, vel,
    z_out, gram_out,
    halo_rates, halo_precond, halo_fields, strips, inject_ref, inject_s,
    state_ring, state_ring_s, damp_ref, damp_s, v_ref, v_s, ring, ring_s,
    split_high, split_low, *, row_count, flip,
):
    count, rows, _ = state.shape
    own = rows // 8
    tiles = own + 1
    odd = odd_part(flip)
    position = lax.axis_index("row")
    above, below = position > 0, position < row_count - 1
    up_a = odd == 0
    keep_a = jnp.where(up_a, above, below).astype(F32)
    keep_b = jnp.where(up_a, below, above).astype(F32)
    near_a, far_a = 6 * (1 - odd), 5 * (1 - odd) + 2 * odd
    near_b, far_b = 6 * odd, 5 * odd + 2 * (1 - odd)
    raws = ((raw_a, near_a, keep_a), (raw_b, near_b, keep_b))
    lates = ((got_a, near_a, keep_a), (got_b, near_b, keep_b))
    blank = jnp.zeros((8, LANES), F32)

    def receive(target, at, sources, index, masked=False):
        for source, near, keep in sources:
            value = source[index]
            target[pl.ds(at + near, 2), :] = value * keep if masked else value

    base = 0
    for halo in (halo_rates, halo_precond):
        for k in range(count * count):
            receive(halo.at[k], 0, raws, base)
            base += 1
    for f in range(3):
        for s in range(count):
            halo_fields[f, s] = blank
            receive(halo_fields.at[f, s], 0, raws, base, f == 0)
            base += 1
    base = 2 * count + 4
    for g in range(base):
        strips[g, 0:rows, :] = strips_in[g]
        strips[g, rows : rows + 8, :] = blank
        receive(strips.at[g], rows, lates, g, g in (2 * count, 2 * count + 3))
    single = [halo_fields.at[0, s] for s in range(count)]
    for k in range(2):
        for s in range(count):
            inject_ref[k, s] = blank
            single.append(inject_ref.at[k, s])
    single.append(strips.at[2 * count, rows : rows + 8])
    for k in range(2):
        inject_s[k] = blank
        single.append(inject_s.at[k])
    for j, target in enumerate(single):
        for source, far, keep in ((got_a, far_a, keep_a), (got_b, far_b, keep_b)):
            row = source[base + j // 2, pl.ds(j % 2, 1), :]
            target[pl.ds(far, 1), :] = row * keep

    speed = speeds(vel, count)
    for n in range(tiles):
        for s in range(count):
            value = state[s, tile_rows(n), :] if n < own else halo_fields[0, s]
            state_ring.at[s][tile_rows(n), :] = value
        state_ring_s[tile_rows(n), :] = strips[2 * count, tile_rows(n), :]

    def putter(main, strip, n):
        def put(s, value):
            if s is None:
                strip[tile_rows(n), :] = value
            else:
                main[s, tile_rows(n), :] = value

        return put

    def getter(main, strip, n):
        return lambda s: strip[tile_rows(n), :] if s is None else main[s, tile_rows(n), :]

    def tile_of(block, halo, n):
        if n < own:
            return lambda s, t: block[s, t, tile_rows(n), :]
        return lambda s, t: halo[s * count + t]

    for n in range(tiles):
        plane = lambda ref, f: (
            (lambda s: ref[s, tile_rows(n), :]) if n < own else (lambda s: halo_fields[f, s])
        )
        first_vector(
            n, state_ring, state_ring_s, plane(quadratic, 1), plane(history, 2),
            tile_of(rates, halo_rates, n), strips, speed, count,
            putter(v_ref.at[0], v_s.at[0], n), putter(damp_ref, damp_s, n),
        )

    own_tiles = [(s, tile_rows(n)) for s in range(count) for n in range(own)]
    high, low, largest = {}, {}, []

    def gram_column(k):
        most = blank
        for s, at in own_tiles:
            value = v_ref[k, s, at, :]
            split_high[k, s, at, :], split_low[k, s, at, :] = split(value)
            most = jnp.maximum(most, jnp.abs(value))
        most = jnp.max(jnp.max(most, axis=0, keepdims=True), axis=1, keepdims=True)
        largest.append(jnp.broadcast_to(most, (8, LANES)))
        for i in range(k + 1):
            start = 64.0 * (largest[i] * largest[k])
            total, lost = start, blank
            for s, at in own_tiles:
                a = split_high[i, s, at, :]
                product = a * split_high[k, s, at, :]
                rest = a * split_low[k, s, at, :] + split_low[i, s, at, :] * v_ref[k, s, at, :]
                after = total + product
                lost = lost + ((product - (after - total)) + rest)
                total = after
            high[i, k], low[i, k] = total - start, lost

    gram_column(0)
    row = row_of(8)
    inside = ((row < 2) & below) | ((row > 5) & above)
    for k in range(KRYLOV):
        last = k == KRYLOV - 1
        pick = min(k, 1)
        for n in range(tiles):
            v = [v_ref[k, s, tile_rows(n), :] for s in range(count)]
            z = products(tile_of(precond, halo_precond, n), v)
            for s in range(count):
                if n < own:
                    z_out[k, s, tile_rows(n), :] = z[s]
                else:
                    z[s] = jnp.where(inside, z[s], inject_ref[pick, s])
                ring.at[s][tile_rows(n), :] = z[s]
            if n < own or not last:
                z_s = strip_product(strips, count, n, v_s[k, tile_rows(n), :], count)
                if n >= own:
                    z_s = jnp.where(inside, z_s, inject_s[pick])
                ring_s[tile_rows(n), :] = z_s
        for n in range(own if last else tiles):
            next_vector(
                n, ring, ring_s, getter(v_ref.at[k], v_s.at[k], n),
                tile_of(rates, halo_rates, n), strips, speed, count,
                putter(v_ref.at[k + 1], v_s.at[k + 1], n), getter(damp_ref, damp_s, n),
                not last,
            )
        gram_column(k + 1)

    row16, lane16 = row_of(16), lane_of(16)
    packs = [jnp.zeros((16, LANES), F32)] * 3
    for n, (i, j) in enumerate(pairs_of(KRYLOV + 1)):
        unit = largest[i] * largest[j]
        coarse, fine = 65536.0 * unit, 8.0 * unit
        first = (high[i, j] + coarse) - coarse
        rest = high[i, j] - first
        second = (rest + fine) - fine
        parts = [first, second, (rest - second) + low[i, j]]
        for shift in (4, 2, 1):
            parts = [x + roll_rows(x, shift) for x in parts]
        packs = [
            jnp.where(row16 == n, jnp.concatenate([x, x], axis=0), pack)
            for x, pack in zip(parts, packs)
        ]
    sums = [jnp.broadcast_to(jnp.sum(x, axis=1, keepdims=True), (16, LANES)) for x in packs]
    top, bottom = two_sum(sums[0], sums[1])
    top, bottom = quick_sum(top, bottom + sums[2])
    line = jnp.where(row16 == lane16, top, 0.0) + jnp.where(row16 + 16 == lane16, bottom, 0.0)
    line = line[:8] + line[8:]
    for shift in (4, 2, 1):
        line = line + roll_rows(line, shift)
    for r in range(0, gram_out.shape[0], 8):
        gram_out[r : r + 8, :] = line


def small_problem(gram):
    width = KRYLOV + 1
    work = dict(gram)
    unit = {}
    pivot = []
    for k in range(width):
        dh, dl = work[k, k]
        pivot.append(jnp.maximum(dh, 0.0))
        inverse = jnp.where(dh > 0.0, 1.0 / jnp.where(dh > 0.0, dh, 1.0), 0.0)
        factor = {}
        for i in range(k + 1, width):
            sh, sl = work[k, i]
            q = sh * inverse
            p, e = two_prod(q, dh)
            rest = ((sh - p) - e) + (sl - q * dl)
            factor[i] = quick_sum(q, rest * inverse)
            unit[k, i] = factor[i][0]
        for i in range(k + 1, width):
            for j in range(i, width):
                fh, fl = factor[i]
                sh, sl = work[k, j]
                p, e = two_prod(fh, sh)
                e = e + (fh * sl + fl * sh)
                wh, wl = work[i, j]
                h, error = two_sum(wh, -p)
                work[i, j] = quick_sum(h, error + (wl - e))
    norm = [jnp.sqrt(d) for d in pivot]
    back = [jnp.where(n > 0.0, 1.0 / jnp.where(n > 0.0, n, 1.0), 0.0) for n in norm]
    inv = {}
    for j in range(KRYLOV):
        inv[j, j] = back[j]
        for i in reversed(range(j)):
            total = unit[i, j] * back[j]
            for m in range(i + 1, j):
                total = total + unit[i, m] * inv[m, j]
            inv[i, j] = -total
    arnoldi = {}
    for j in range(KRYLOV):
        shifted = [inv[0, j]]
        for i in range(1, j + 1):
            shifted.append(inv[i, j] + inv[i - 1, j])
        shifted.append(inv[j, j])
        for i in range(j + 2):
            total = shifted[i]
            for m in range(i + 1, j + 2):
                total = total + unit[i, m] * shifted[m]
            arnoldi[i, j] = norm[i] * total
    beta = jnp.sqrt(pivot[0] + tiny_eps)
    basis = [[norm[0] / beta]]
    hessen = {}
    for k in range(KRYLOV):
        vector = []
        for i in range(k + 2):
            terms = [arnoldi[i, j] * basis[k][j] for j in range(max(i - 1, 0), k + 1)]
            vector.append(functools.reduce(jnp.add, terms))
        for i in range(k + 1):
            terms = [a * b for a, b in zip(basis[i], vector)]
            hessen[i, k] = functools.reduce(jnp.add, terms)
        for m in range(k + 1):
            terms = [hessen[i, k] * basis[i][m] for i in range(m, k + 1)]
            vector[m] = vector[m] - functools.reduce(jnp.add, terms)
        squared = functools.reduce(jnp.add, [x * x for x in vector])
        size = jnp.sqrt(squared + tiny_eps)
        hessen[k + 1, k] = size
        basis.append([x / size for x in vector])
    rotated = [beta] + [jnp.zeros_like(beta)] * KRYLOV
    for k in range(KRYLOV):
        first, second = hessen[k, k], hessen[k + 1, k]
        radius = jnp.sqrt(first * first + second * second)
        cosine, sine = first / radius, second / radius
        for j in range(k, KRYLOV):
            upper = hessen[k, j]
            under = hessen.get((k + 1, j))
            hessen[k, j] = cosine * upper + sine * under
            hessen[k + 1, j] = cosine * under - sine * upper
        rotated[k], rotated[k + 1] = (
            cosine * rotated[k] + sine * rotated[k + 1],
            cosine * rotated[k + 1] - sine * rotated[k],
        )
    coef = [None] * KRYLOV
    for k in reversed(range(KRYLOV)):
        total = rotated[k]
        for j in range(k + 1, KRYLOV):
            total = total - hessen[k, j] * coef[j]
        coef[k] = total / hessen[k, k]
    in_q = [
        functools.reduce(jnp.add, [coef[k] * basis[k][m] for k in range(m, KRYLOV)])
        for m in range(KRYLOV)
    ]
    in_v = [
        functools.reduce(jnp.add, [inv[i, j] * in_q[j] for j in range(i, KRYLOV)])
        for i in range(KRYLOV)
    ]
    return in_v, jnp.abs(rotated[KRYLOV])


def solve_kernel(gathered, z_ref, state, updated, residual):
    count, rows, _ = state.shape
    high = gathered[0:8, :]
    low = roll_lanes(high, -16)
    for r in range(8, gathered.shape[0], 8):
        tile = gathered[r : r + 8, :]
        high, error = two_sum(high, tile)
        low = low + roll_lanes(tile, -16) + error
    for shift in (4, 2, 1):
        high, error = two_sum(high, roll_rows(high, shift))
        low = low + roll_rows(low, shift) + error
    high, low = quick_sum(high, low)
    gram = {}
    for n, pair in enumerate(pairs_of(KRYLOV + 1)):
        gram[pair] = (
            jnp.broadcast_to(high[:, n : n + 1], (8, LANES)),
            jnp.broadcast_to(low[:, n : n + 1], (8, LANES)),
        )
    weights, last = small_problem(gram)
    for s in range(count):
        for r in range(0, rows, 8):
            total = weights[0] * z_ref[0, s, r : r + 8, :]
            for k in range(1, KRYLOV):
                total = total + weights[k] * z_ref[k, s, r : r + 8, :]
            updated[s, r : r + 8, :] = state[s, r : r + 8, :] + total
    residual[0] = last[0, 0]


def closed_chain(parts, size, flip):
    chain = []
    for p in range(parts):
        for r in range(size):
            if flip and p % 2:
                target = (p, r - 1) if r else (p - 1, 0)
            elif flip:
                target = (p, r + 1) if r < size - 1 else (p + 1, r)
            else:
                target = (p, (r + 1) % size)
            chain.append((p * size + r, target[0] * size + target[1]))
    return chain, [(b, a) for a, b in chain]


def shapes(*dims):
    return jax.ShapeDtypeStruct(dims, F32)


def body(state, history, rates, quadratic, velocity, precond):
    count, rows, _ = state.shape
    part_count = lax.axis_size("parts")
    row_count = lax.axis_size("row")
    col_count = lax.axis_size("col")
    flip = part_count % 2 == 0
    block = (count, rows, LANES)

    square = (count,) + block
    smem = pl.BlockSpec(memory_space=pltpu.SMEM)
    whole = pl.BlockSpec(memory_space=pltpu.VMEM)
    inputs = [
        pltpu.with_memory_space_constraint(x, pltpu.HBM)
        for x in (state, history, rates, quadratic, precond)
    ]
    (
        state, history, rates, quadratic, precond, edge_a, edge_b, send_a, send_b
    ) = pl.pallas_call(
        functools.partial(pack_kernel, flip=flip),
        in_specs=[pl.BlockSpec(memory_space=pltpu.HBM)] * 5,
        out_shape=[
            shapes(*block), shapes(*block), shapes(*square), shapes(*block), shapes(*square),
            shapes(count + 2, rows, LANES), shapes(count + 2, rows, LANES),
            shapes(raw_planes(count), 2, LANES), shapes(raw_planes(count), 2, LANES),
        ],
        out_specs=[whole] * 9,
        scratch_shapes=[pltpu.SemaphoreType.DMA((5,))],
        compiler_params=VMEM,
        name="pack_columns",
    )(*inputs)
    down, up = closed_chain(part_count, row_count, flip)
    right, left = closed_chain(part_count, col_count, False)
    got_a = lax.ppermute(edge_a, ("parts", "col"), right)
    got_b = lax.ppermute(edge_b, ("parts", "col"), left)
    raw_a = lax.ppermute(send_a, ("parts", "row"), down)
    raw_b = lax.ppermute(send_b, ("parts", "row"), up)

    planes = message_planes(count)
    strips, send_a, send_b = pl.pallas_call(
        functools.partial(half_kernel, counts=(col_count, flip)),
        in_specs=[whole] * 8,
        out_shape=[shapes(2 * count + 4, rows, LANES)] + [shapes(planes, 2, LANES)] * 2,
        scratch_shapes=[
            pltpu.VMEM((count, rows, LANES), F32),
            pltpu.VMEM((rows, LANES), F32),
            pltpu.VMEM(block, F32),
            pltpu.VMEM((rows, LANES), F32),
            pltpu.VMEM(block, F32),
            pltpu.VMEM((rows, LANES), F32),
            pltpu.VMEM((2, count, rows, LANES), F32),
            pltpu.VMEM((2, rows, LANES), F32),
        ],
        compiler_params=VMEM,
        name="half_step",
    )(got_a, got_b, state, history, rates, quadratic, precond, velocity)

    got_a = lax.ppermute(send_a, ("parts", "row"), down)
    got_b = lax.ppermute(send_b, ("parts", "row"), up)

    ext = rows + 8
    members = row_count * col_count
    z, gram = pl.pallas_call(
        functools.partial(full_kernel, row_count=row_count, flip=flip),
        in_specs=[whole] * 11,
        out_shape=[shapes(KRYLOV, *block), shapes(members, LANES)],
        scratch_shapes=[
            pltpu.VMEM((count * count, 8, LANES), F32),
            pltpu.VMEM((count * count, 8, LANES), F32),
            pltpu.VMEM((3, count, 8, LANES), F32),
            pltpu.VMEM((2 * count + 4, ext, LANES), F32),
            pltpu.VMEM((2, count, 8, LANES), F32),
            pltpu.VMEM((2, 8, LANES), F32),
            pltpu.VMEM((count, ext, LANES), F32),
            pltpu.VMEM((ext, LANES), F32),
            pltpu.VMEM((count, ext, LANES), F32),
            pltpu.VMEM((ext, LANES), F32),
            pltpu.VMEM((KRYLOV + 1, count, ext, LANES), F32),
            pltpu.VMEM((KRYLOV + 1, ext, LANES), F32),
            pltpu.VMEM((count, ext, LANES), F32),
            pltpu.VMEM((ext, LANES), F32),
            pltpu.VMEM((KRYLOV + 1,) + block, F32),
            pltpu.VMEM((KRYLOV + 1,) + block, F32),
        ],
        compiler_params=VMEM,
        name="krylov",
    )(raw_a, raw_b, got_a, got_b, strips, state, history, rates, quadratic, precond, velocity)

    gathered = lax.all_to_all(gram, ("row", "col"), 0, 0, tiled=True)
    updated, last = pl.pallas_call(
        solve_kernel,
        out_shape=[shapes(*block), shapes(1)],
        out_specs=[whole, smem],
        compiler_params=VMEM,
        name="solve",
    )(gathered, z, state)
    return updated, last


def solution(mesh):
    placed = (
        P(None, ("parts", "row"), "col"),
        P(None, ("parts", "row"), "col"),
        P(None, None, ("parts", "row"), "col"),
        P(None, ("parts", "row"), "col"),
        P(),
        P(None, None, ("parts", "row"), "col"),
    )
    return jax.shard_map(
        body,
        mesh=mesh,
        in_specs=placed,
        out_specs=(P(None, ("parts", "row"), "col"), P("parts")),
        check_vma=False,
    )
```

time: 34.7 us -> 33.4 us (0.963)
  Pallas kernels: 8.21 us -> 6.83 us
    pallas_call x1, Pallas kernels: 3.72 us -> 2.51 us  [body(): pl.pallas_call(functools.partial(full_kernel, row_count=row_count, flip=f...]
  transfers between devices with their start and end apart: 6 -> 6, of which waited for: 4 -> 4; matrix products, arithmetic and copies ran while one was open for 0% -> 0% of each run, Pallas kernels for 3% -> 2%
where the time goes in v5:
time: 33.4 us; the launch traced here: 33.2 us
  blocking collectives  12.4 us (37%)
  starting transfers between devices  6.94 us (21%)
  Pallas kernels  6.83 us (20%)
  waiting for transfers between devices  6.27 us (19%)
  between operations  0.65 us (2%)
    all_to_all x1, blocking collectives, body(): gathered = lax.all_to_all(gram, ('row', 'col'), 0, 0, tiled=True)  12.4 us
    ppermute x1, starting transfers between devices, body(): raw_a = lax.ppermute(send_a, ('parts', 'row'), down)  3.1 us
    pallas_call x1, Pallas kernels, body(): pl.pallas_call(functools.partial(full_kernel, row_count=row_count, flip=f...  2.51 us
    pallas_call x1, Pallas kernels, body(): pl.pallas_call(functools.partial(pack_kernel, flip=flip), in_specs=[pl.Bl...  2.44 us
    ppermute x1, waiting for transfers between devices, body(): got_a = lax.ppermute(edge_a, ('parts', 'col'), right)  2.2 us
    ppermute x1, waiting for transfers between devices, body(): got_a = lax.ppermute(send_a, ('parts', 'row'), down)  1.99 us
    ppermute x1, starting transfers between devices, body(): got_b = lax.ppermute(edge_b, ('parts', 'col'), left)  1.74 us
    ppermute x1, starting transfers between devices, body(): got_a = lax.ppermute(send_a, ('parts', 'row'), down)  1.63 us
  transfers between devices with their start and end apart: 6, of which 4 were waited for; matrix products, arithmetic and copies ran while one was open for 0% of the time, Pallas kernels for 2%

profile of v5, /device:TPU:0, one launch (start us, length us, event | category | flops | bytes accessed | tf_op | source)
XLA Modules:
  0.0 33.2 jit_solution(1381791087876028124)
XLA Ops:
  0.6 2.4 %pack_columns.1 = (f32[10,16,128]{2,1,0:T(8,128)S(1)}, f32[10,16,128]{2,1,0:T(8,128)S(1)}, f32[10,10,16,128]{3,2,1,0:T(8,128)S(1)}, f32[10,16,128]{2,1,0:T(8,128...) custom-call(f32[10,16,128]{2,1,0:T(8,128)} %state_in.1, ...), custom_call_target="tpu_custom_call" | custom-call | tf_op jit(solution)/shard_map/pack_columns/pallas_call | solution.py:659
  3.1 3.1 %collective-permute-start = (f32[230,2,128]{2,1,0:T(2,128)S(1)}, f32[230,2,128]{2,1,0:T(2,128)S(1)}, u32[]{:S(2)}, u32[]{:S(2)}) collective-permute-start(f32[230,2,128]{2,1,0:T(2,128)S(1)} %get-tuple-element.16), channel_id=1, source_target_pairs={{0,4},{4,8},{8,12},{12,28},{16,0},{20,16},{24,20},{28,24},{1,5},{5... | collective-permute-start | bytes 706568 | tf_op jit(solution)/shard_map/ppermute | solution.py:676
  6.2 0.0 collective-permute-start.1
  6.2 0.0 copy-start
  6.2 0.0 collective-permute-start.2
  6.2 1.7 %collective-permute-start.3 = (f32[12,16,128]{2,1,0:T(8,128)S(1)}, f32[12,16,128]{2,1,0:T(8,128)S(1)}, u32[]{:S(2)}, u32[]{:S(2)}) collective-permute-start(f32[12,16,128]{2,1,0:T(8,128)S(1)} %get-tuple-element.19), channel_id=1, source_target_pairs={{1,0},{2,1},{3,2},{0,3},{17,16},{18,17},{19,18},{16,19},{5,4},{6,5... | collective-permute-start | bytes 294920 | tf_op jit(solution)/shard_map/ppermute | solution.py:675
  7.9 0.0 copy-done
  8.0 0.1 copy.10.vel
  8.0 2.2 %collective-permute-done.2.edge_a = f32[12,16,128]{2,1,0:T(8,128)S(1)} collective-permute-done((f32[12,16,128]{2,1,0:T(8,128)S(1)}, f32[12,16,128]{2,1,0:T(8,128)S(1)}, u32[]{:S(2)}, u32[]{:S(2)}) %collective-permute-start.2) | collective-permute-done | bytes 98336 | tf_op jit(solution)/shard_map/ppermute | solution.py:674
  10.2 0.5 %collective-permute-done.3.edge_b = f32[12,16,128]{2,1,0:T(8,128)S(1)} collective-permute-done((f32[12,16,128]{2,1,0:T(8,128)S(1)}, f32[12,16,128]{2,1,0:T(8,128)S(1)}, u32[]{:S(2)}, u32[]{:S(2)}) %collective-permute-start.3) | collective-permute-done | bytes 98336 | tf_op jit(solution)/shard_map/ppermute | solution.py:675
  10.7 0.8 %half_step.1 = (f32[24,16,128]{2,1,0:T(8,128)S(1)}, f32[41,2,128]{2,1,0:T(2,128)S(1)}, f32[41,2,128]{2,1,0:T(2,128)S(1)}) custom-call(f32[12,16,128]{2,1,0:T(8,128)S(1)} %collective-permute-done.2.edge_a, f32[12,16,128]{2,1,0:T(8,128)S(1)} %collective-permute-done.3.edge_b, f32[10,16,128]{2,1,0:T(8,128)S(1)} %get-tuple-element.20.state, ...), custom_call_target="tpu_custom_call" | custom-call | tf_op jit(solution)/shard_map/half_step/pallas_call | solution.py:680
  11.5 1.6 %collective-permute-start.4 = (f32[41,2,128]{2,1,0:T(2,128)S(1)}, f32[41,2,128]{2,1,0:T(2,128)S(1)}, u32[]{:S(2)}, u32[]{:S(2)}) collective-permute-start(f32[41,2,128]{2,1,0:T(2,128)S(1)} %get-tuple-element.25), channel_id=1, source_target_pairs={{0,4},{4,8},{8,12},{12,28},{16,0},{20,16},{24,20},{28,24},{1,5},{5... | collective-permute-start | bytes 125960 | tf_op jit(solution)/shard_map/ppermute | solution.py:698
  13.1 0.4 %collective-permute-start.5 = (f32[41,2,128]{2,1,0:T(2,128)S(1)}, f32[41,2,128]{2,1,0:T(2,128)S(1)}, u32[]{:S(2)}, u32[]{:S(2)}) collective-permute-start(f32[41,2,128]{2,1,0:T(2,128)S(1)} %get-tuple-element.26), channel_id=1, source_target_pairs={{4,0},{8,4},{12,8},{28,12},{0,16},{16,20},{20,24},{24,28},{5,1},{9... | collective-permute-start | bytes 125960 | tf_op jit(solution)/shard_map/ppermute | solution.py:699
  13.6 2.0 %collective-permute-done.4.got_a = f32[41,2,128]{2,1,0:T(2,128)S(1)} collective-permute-done((f32[41,2,128]{2,1,0:T(2,128)S(1)}, f32[41,2,128]{2,1,0:T(2,128)S(1)}, u32[]{:S(2)}, u32[]{:S(2)}) %collective-permute-start.4) | collective-permute-done | bytes 42016 | tf_op jit(solution)/shard_map/ppermute | solution.py:698
  15.6 1.6 %collective-permute-done.5.got_b = f32[41,2,128]{2,1,0:T(2,128)S(1)} collective-permute-done((f32[41,2,128]{2,1,0:T(2,128)S(1)}, f32[41,2,128]{2,1,0:T(2,128)S(1)}, u32[]{:S(2)}, u32[]{:S(2)}) %collective-permute-start.5) | collective-permute-done | bytes 42016 | tf_op jit(solution)/shard_map/ppermute | solution.py:699
  17.2 0.0 collective-permute-done.raw_a
  17.2 0.0 collective-permute-done.1.raw_b
  17.2 2.5 %krylov.1 = (f32[4,10,16,128]{3,2,1,0:T(8,128)S(1)}, f32[16,128]{1,0:T(8,128)S(1)}) custom-call(f32[230,2,128]{2,1,0:T(2,128)S(1)} %collective-permute-done.raw_a, f32[230,2,128]{2,1,0:T(2,128)S(1)} %collective-permute-done.1.raw_b, f32[41,2,128]{2,1,0:T(2,128)S(1)} %collective-permute-done.4.got_a, f32[41,2,128]{2,1,0:T(2,128)S(1)} %collective-permute-done.5.got_b, ...), custom_call_target="tpu_custom_call" | custom-call | tf_op jit(solution)/shard_map/krylov/pallas_call | solution.py:703
  19.7 12.4 %all_to_all.11 = f32[16,1,128]{2,1,0:T(1,128)S(1)} all-to-all(f32[16,1,128]{2,1,0:T(1,128)S(1)} %bitcast.5), channel_id=1, replica_groups=mesh['parts'=2,'row'=4,'col'=4] {'row','col'}, dimensions={0} | all-to-all | bytes 16384 | tf_op jit(solution)/shard_map/all_to_all | solution.py:729
  32.1 1.1 %solve.1 = (f32[10,16,128]{2,1,0:T(8,128)}, f32[1]{0:T(128)}) custom-call(f32[16,128]{1,0:T(8,128)S(1)} %bitcast.4, f32[4,10,16,128]{3,2,1,0:T(8,128)S(1)} %get-tuple-element.29.z_ref, f32[10,16,128]{2,1,0:T(8,128)S(1)} %get-tuple-element.20.state), custom_call_target="tpu_custom_call" | custom-call | tf_op jit(solution)/shard_map/solve/pallas_call | solution.py:730
Async XLA Ops:
  3.1 14.1 %collective-permute-start = (f32[230,2,128]{2,1,0:T(2,128)S(1)}, f32[230,2,128]{2,1,0:T(2,128)S(1)}, u32[]{:S(2)}, u32[]{:S(2)}) collective-permute-start(f32[230,2,128]{2,1,0:T(2,128)S(1)} %get-tuple-element.16), channel_id=1, source_target_pairs={{0,4},{4,8},{8,12},{12,28},{16,0},{20,16},{24,20},{28,24},{1,5},{5... | collective-permute-start | bytes 706568 | tf_op jit(solution)/shard_map/ppermute | solution.py:676
  6.2 11.0 %collective-permute-start.1 = (f32[230,2,128]{2,1,0:T(2,128)S(1)}, f32[230,2,128]{2,1,0:T(2,128)S(1)}, u32[]{:S(2)}, u32[]{:S(2)}) collective-permute-start(f32[230,2,128]{2,1,0:T(2,128)S(1)} %get-tuple-element.17), channel_id=1, source_target_pairs={{4,0},{8,4},{12,8},{28,12},{0,16},{16,20},{20,24},{24,28},{5,1},{9... | collective-permute-start | bytes 706568 | tf_op jit(solution)/shard_map/ppermute | solution.py:677
  6.2 1.8 %copy-start = (f32[10,2]{0,1:T(2,128)S(1)}, f32[10,2]{0,1:T(2,128)}, u32[]{:S(2)}) copy-start(f32[10,2]{0,1:T(2,128)} %param.10) | copy-start | bytes 244
  6.2 4.0 %collective-permute-start.2 = (f32[12,16,128]{2,1,0:T(8,128)S(1)}, f32[12,16,128]{2,1,0:T(8,128)S(1)}, u32[]{:S(2)}, u32[]{:S(2)}) collective-permute-start(f32[12,16,128]{2,1,0:T(8,128)S(1)} %get-tuple-element.18), channel_id=1, source_target_pairs={{0,1},{1,2},{2,3},{3,0},{16,17},{17,18},{18,19},{19,16},{4,5},{5,6... | collective-permute-start | bytes 294920 | tf_op jit(solution)/shard_map/ppermute | solution.py:674
  6.2 4.5 %collective-permute-start.3 = (f32[12,16,128]{2,1,0:T(8,128)S(1)}, f32[12,16,128]{2,1,0:T(8,128)S(1)}, u32[]{:S(2)}, u32[]{:S(2)}) collective-permute-start(f32[12,16,128]{2,1,0:T(8,128)S(1)} %get-tuple-element.19), channel_id=1, source_target_pairs={{1,0},{2,1},{3,2},{0,3},{17,16},{18,17},{19,18},{16,19},{5,4},{6,5... | collective-permute-start | bytes 294920 | tf_op jit(solution)/shard_map/ppermute | solution.py:675
  11.5 4.1 %collective-permute-start.4 = (f32[41,2,128]{2,1,0:T(2,128)S(1)}, f32[41,2,128]{2,1,0:T(2,128)S(1)}, u32[]{:S(2)}, u32[]{:S(2)}) collective-permute-start(f32[41,2,128]{2,1,0:T(2,128)S(1)} %get-tuple-element.25), channel_id=1, source_target_pairs={{0,4},{4,8},{8,12},{12,28},{16,0},{20,16},{24,20},{28,24},{1,5},{5... | collective-permute-start | bytes 125960 | tf_op jit(solution)/shard_map/ppermute | solution.py:698
  13.1 4.0 %collective-permute-start.5 = (f32[41,2,128]{2,1,0:T(2,128)S(1)}, f32[41,2,128]{2,1,0:T(2,128)S(1)}, u32[]{:S(2)}, u32[]{:S(2)}) collective-permute-start(f32[41,2,128]{2,1,0:T(2,128)S(1)} %get-tuple-element.26), channel_id=1, source_target_pairs={{4,0},{8,4},{12,8},{28,12},{0,16},{16,20},{20,24},{24,28},{5,1},{9... | collective-permute-start | bytes 125960 | tf_op jit(solution)/shard_map/ppermute | solution.py:699
